TPU v7x, 32 devices: a whole 2x2x4 slice. The times are simulated.
32 devices in a mesh: row: 16 (over z, y, core), col: 2 (over x).
Axes of the slice: x: 2, y: 2, z: 4, core: 2. Of those that a mesh axis runs over, the one named last changes fastest.
Arguments:
- inputs: bfloat16 [1536, 1024], P(('row', 'col')), may hold values from -6 to 6
- first_weight: bfloat16 [1024, 1024], replicated, may hold values from -0.1875 to 0.1875
- second_weight: bfloat16 [1024, 1024], replicated, may hold values from -0.1875 to 0.1875
- readout: bfloat16 [1024], replicated, may hold values from -0.1875 to 0.1875
- target: float32 [1536], P(('row', 'col')), may hold values from -6 to 6
- counts: int32 [1536], P(('row', 'col')), may hold values from 1 to 32, as said below
- views: int32 [1536], P(('row', 'col')), may hold values from 0 to 1999
Outputs:
- update: float32 [1024, 2048], P(('row', 'col'))
Inputs may be any that keep to these rules, and one draw needn't show every extreme that they name: `counts`: number of samples taken along the ray.
All inputs are finite; a program needn't handle non-finite values.
Results may differ from a plain program's by a relative error of at most 0.008.
Values may be sent and summed in bfloat16 or wider, within the bound.
No kernel may reach another device: no remote copies, remote signals or barrier semaphores. Data moves between devices by JAX's collectives and lax.ppermute only.
A program may use at most 128 MiB of HBM per device.

v0:
```python
import jax
import jax.numpy as jnp
from jax import lax
from jax.experimental import pallas as pl
from jax.experimental.pallas import tpu as pltpu
from jax.sharding import PartitionSpec as P


VIEWS = 2000
ITERS = 3


DAMP = 4.0
LEARN = 8.0
HIGH = lax.Precision.HIGHEST
LANES = 128
BLOCK = 256
VMEM_BYTES = 30 * 2**20


def slope(value):
    sig = jax.nn.sigmoid(value)
    return sig * (1.0 + value * (1.0 - sig))


def ray_weight(counts, views):
    angle = 2.0 * jnp.pi / VIEWS * views.astype(jnp.float32)
    return counts.astype(jnp.float32) / 16.0 * (1.0 + 0.5 * jnp.cos(angle))


def carry_back(outer_grad, second_weight, pre_first):
    carried = lax.dot_general(
        outer_grad, second_weight, (((1,), (1,)), ((), ())), preferred_element_type=jnp.float32
    )
    return (carried * slope(pre_first)).astype(jnp.bfloat16)


def gram(left, other):
    return lax.dot_general(
        left, other, (((1,), (1,)), ((), ())), preferred_element_type=jnp.float32
    )


def global_sums(values):
    return lax.psum((values[0], values[1]), ("row", "col"))


def shards(inputs, first_weight, second_weight, readout, target, counts, views):
    weight_rows = ray_weight(counts, views)
    pre_first = jnp.dot(inputs, first_weight, preferred_element_type=jnp.float32)
    hidden = jax.nn.silu(pre_first).astype(jnp.bfloat16)
    pre_second = jnp.dot(hidden, second_weight, preferred_element_type=jnp.float32)
    readout_f = readout.astype(jnp.float32)
    signal = jnp.sum(jax.nn.silu(pre_second) * readout_f[None, :], axis=1)
    right = weight_rows * signal - target
    outer_grad = (weight_rows[:, None] * slope(pre_second) * readout_f[None, :]).astype(
        jnp.bfloat16
    )
    inner_grad = carry_back(outer_grad, second_weight, pre_first)
    block_in, block_inner, block_hidden, block_outer = (
        lax.all_gather(inputs, "col", axis=0, tiled=True),
        lax.all_gather(inner_grad, "col", axis=0, tiled=True),
        lax.all_gather(hidden, "col", axis=0, tiled=True),
        lax.all_gather(outer_grad, "col", axis=0, tiled=True),
    )
    cross_in, cross_inner, cross_hidden, cross_outer = (
        lax.all_gather(inputs, "row", axis=0, tiled=True),
        lax.all_gather(inner_grad, "row", axis=0, tiled=True),
        lax.all_gather(hidden, "row", axis=0, tiled=True),
        lax.all_gather(outer_grad, "row", axis=0, tiled=True),
    )
    kernel = gram(block_in, cross_in) * gram(block_inner, cross_inner)
    kernel = kernel + gram(block_hidden, cross_hidden) * gram(block_outer, cross_outer)

    def apply(direction):
        spread = lax.all_gather(direction, "row", axis=0, tiled=True)
        partial_value = jnp.dot(kernel, spread, precision=HIGH, preferred_element_type=jnp.float32)
        own = lax.psum_scatter(partial_value, "col", scatter_dimension=0, tiled=True)
        return own + DAMP * direction

    solution = jnp.zeros_like(right)
    residual = right
    image = apply(residual)
    norm_now, product = global_sums((jnp.sum(residual * residual), jnp.sum(residual * image)))
    alpha = norm_now / product
    direction, along = (residual, image)
    for step in range(ITERS):
        solution = solution + alpha * direction
        residual = residual - alpha * along
        if step + 1 < ITERS:
            image = apply(residual)
            norm_next, product = global_sums(
                (jnp.sum(residual * residual), jnp.sum(residual * image))
            )
            ratio = norm_next / norm_now
            alpha = norm_next / (product - ratio * norm_next / alpha)
            direction = residual + ratio * direction
            along = image + ratio * along
            norm_now = norm_next
    weighted_inner = solution[:, None] * inner_grad.astype(jnp.float32)
    weighted_outer = solution[:, None] * outer_grad.astype(jnp.float32)
    inputs_f = inputs.astype(jnp.float32)
    hidden_f = hidden.astype(jnp.float32)
    first = lax.dot_general(
        inputs_f,
        weighted_inner,
        (((0,), (0,)), ((), ())),
        precision=HIGH,
        preferred_element_type=jnp.float32,
    )
    second = lax.dot_general(
        hidden_f,
        weighted_outer,
        (((0,), (0,)), ((), ())),
        precision=HIGH,
        preferred_element_type=jnp.float32,
    )
    return lax.psum_scatter(
        -LEARN * jnp.concatenate([first, second], axis=1),
        ("row", "col"),
        scatter_dimension=0,
        tiled=True,
    )


def bdot(left, right, contract):
    return lax.dot_general(left, right, (contract, ((), ())), preferred_element_type=jnp.float32)


def sigmoid(value):
    return 1.0 / (1.0 + jnp.exp(-value))


def take(refs, start, size, cols):
    parts, offset = [], 0
    for ref in refs:
        low = max(start - offset, 0)
        high = min(start + size - offset, ref.shape[0])
        if low < high:
            parts.append(ref[low:high, cols])
        offset += ref.shape[0]
    return parts[0] if len(parts) == 1 else jnp.concatenate(parts, axis=0)


def features(pays, w1_ref, w2_ref, ro_ref, hid_ref, grad_ref, inn_ref, right_ref):
    rays, width = hid_ref.shape
    extra = take(pays, 0, rays, slice(width, width + LANES)).astype(jnp.float32)
    weight = extra[:, 0:1] + extra[:, 1:2] + extra[:, 2:3]
    target = extra[:, 3:4] + extra[:, 4:5] + extra[:, 5:6]
    pre = bdot(take(pays, 0, rays, slice(0, width)), w1_ref[...], ((1,), (0,)))
    sig = sigmoid(pre)
    slope_first = sig * (1.0 + pre * (1.0 - sig))
    hidden = (pre * sig).astype(jnp.bfloat16)
    hid_ref[...] = hidden
    pre = bdot(hidden, w2_ref[...], ((1,), (0,)))
    sig = sigmoid(pre)
    readout = ro_ref[...]
    signal = jnp.sum(pre * sig * readout, axis=1, keepdims=True)
    grad = (weight * (sig * (1.0 + pre * (1.0 - sig))) * readout).astype(jnp.bfloat16)
    grad_ref[...] = grad
    carried = bdot(grad, w2_ref[...], ((1,), (1,)))
    inn_ref[...] = (carried * slope_first).astype(jnp.bfloat16)
    right_ref[...] = jnp.broadcast_to(weight * signal - target, (rays, LANES))


def products(first, last, pays, inns, hids, grads, strip_ref, mirror_ref):
    width = hids[0].shape[1]
    whole = slice(0, width)
    nt = ((1,), (1,))

    def pair(refs, r, c):
        return bdot(take(refs, r * BLOCK, BLOCK, whole), take(refs, c * BLOCK, BLOCK, whole), nt)

    for r in range(first, last):
        rows = slice((r - first) * BLOCK, (r - first + 1) * BLOCK)
        for c in range(r + 1):
            value = pair(pays, r, c) * pair(inns, r, c) + pair(hids, r, c) * pair(grads, r, c)
            strip_ref[rows, c * BLOCK : (c + 1) * BLOCK] = value
            if c < first:
                mirror_ref[c * BLOCK : (c + 1) * BLOCK, rows] = value.T
            elif c < r:
                other = slice((c - first) * BLOCK, (c - first + 1) * BLOCK)
                strip_ref[other, r * BLOCK : (r + 1) * BLOCK] = value.T


def finish(pays, inns, hids, grads, rights, strips, mirrors, own, out_ref, col_ref):
    width = hids[0].shape[1]
    total = sum(ref.shape[0] for ref in hids)
    tiles = total // LANES

    def to_columns(row):
        for t in range(tiles):
            piece = jnp.broadcast_to(row[:, t * LANES : (t + 1) * LANES], (8, LANES)).T
            col_ref[t * LANES : (t + 1) * LANES, :] = jnp.broadcast_to(
                piece[:, 0:1], (LANES, LANES)
            )

    def sweep(ref, offset, pieces, place):
        count = ref.shape[1] // LANES
        groups = ref.shape[0] // 8
        many = 1
        while many * count < 24 and groups % (2 * many) == 0:
            many *= 2

        def body(i, sums):
            terms = [[] for _ in range(count)]
            for j in range(many):
                g = i * many + j
                rows = pl.ds(pl.multiple_of(g * 8, 8), 8)
                scale = col_ref[pl.ds(pl.multiple_of(offset + g * 8, 8), 8), :]
                for t in range(count):
                    terms[t].append(ref[rows, t * LANES : (t + 1) * LANES] * scale)
            for values in terms:
                while len(values) > 1:
                    values[:] = [sum(values[k : k + 2]) for k in range(0, len(values), 2)]
            return tuple(a + values[0] for a, values in zip(sums, terms))

        zeros = tuple(jnp.zeros((8, LANES), jnp.float32) for _ in range(count))
        for t, a in enumerate(lax.fori_loop(0, groups // many, body, zeros, unroll=4)):
            k = place + t
            pieces[k] = a if pieces[k] is None else pieces[k] + a

    def apply(row):
        to_columns(row)
        pieces, offset = [None] * tiles, 0
        for strip, mirror in zip(strips, mirrors):
            sweep(strip, offset, pieces, 0)
            if mirror is not None:
                sweep(mirror, 0, pieces, offset // LANES)
            offset += strip.shape[0]
        joined = jnp.concatenate(pieces, axis=1)
        return jnp.sum(joined, axis=0, keepdims=True) + DAMP * row

    def dot(a, b):
        return jnp.sum(a * b, axis=1, keepdims=True)

    right = jnp.concatenate(
        [
            ref[k * LANES : (k + 1) * LANES, :].T[0:1, :]
            for ref in rights
            for k in range(ref.shape[0] // LANES)
        ],
        axis=1,
    )
    answer = jnp.zeros_like(right)
    residual, direction = right, right
    norm_now = dot(right, right)
    for step in range(ITERS):
        image = apply(direction)
        alpha = norm_now / dot(direction, image)
        answer = answer + alpha * direction
        if step + 1 < ITERS:
            residual = residual - alpha * image
            norm_next = dot(residual, residual)
            direction = residual + (norm_next / norm_now) * direction
            norm_now = norm_next
    to_columns(answer)
    rank = lax.axis_index("row") * lax.axis_size("col") + lax.axis_index("col")
    start = rank * own
    base = pl.multiple_of(start // LANES * LANES, LANES)
    shift = (LANES - (start - base)) % LANES
    cols = pl.ds(base, LANES)
    lane = None
    sums = [jnp.zeros((LANES, width), jnp.float32)] * 2
    offset = 0
    for inn_ref, grad_ref, hid_ref in zip(inns, grads, hids):
        rays = hid_ref.shape[0]
        scale = col_ref[offset : offset + rays, :]
        lane = lax.broadcasted_iota(jnp.int32, (rays, LANES), 1)
        lefts = (take(pays, offset, rays, cols), hid_ref[:, cols])
        for which, (left, ref) in enumerate(zip(lefts, (inn_ref, grad_ref))):
            left = pltpu.roll(left.astype(jnp.float32) * scale, shift, 1)
            high = left.astype(jnp.bfloat16).astype(jnp.float32)
            rest = left - high
            middle = rest.astype(jnp.bfloat16).astype(jnp.float32)
            low = rest - middle
            packed = jnp.where(lane < 2 * own, pltpu.roll(middle, own, 1), pltpu.roll(low, 2 * own, 1))
            packed = jnp.where(lane < own, high, packed).astype(jnp.bfloat16)
            sums[which] = sums[which] + bdot(packed, ref[...], ((0,), (0,)))
        offset += rays
    for which, value in enumerate(sums):
        value = value[0:own] + value[own : 2 * own] + value[2 * own : 3 * own]
        out_ref[:, which * width : (which + 1) * width] = -LEARN * value


def stage(k, count, pays, w1, w2, ro, before, own):
    width, units = w1.shape
    rays = sum(a.shape[0] for a in pays)
    first, last = k * rays // BLOCK, (k + 1) * rays // BLOCK
    final = k + 1 == count
    rows, cols = (last - first) * BLOCK, last * BLOCK
    made = [((rays, units), jnp.bfloat16)] * 3 + [((rays, LANES), jnp.float32)]
    made.append(((rows, cols), jnp.float32))
    if first:
        made.append(((first * BLOCK, rows), jnp.float32))
    operands, spots = [], []

    def place(arrays):
        spots.append((len(operands), len(operands) + len(arrays)))
        operands.extend(arrays)

    place([*pays, w1, w2, ro])
    for done in before:
        place(done["pays"])
        place(done["made"] if final else done["made"][:3])

    def kernel(*refs):
        groups = [list(refs[a:b]) for a, b in spots]
        tail = list(refs[len(operands) :])
        out_ref = tail.pop(0) if final else None
        mine = tail[: len(made)]
        own_pays = groups[0][: len(pays)]
        features(own_pays, *groups[0][len(pays) :], *mine[:4])
        old_pays = [ref for group in groups[1::2] for ref in group]
        hids, grads, inns = ([g[i] for g in groups[2::2]] + [mine[i]] for i in range(3))
        every = [*old_pays, *own_pays]
        products(first, last, every, inns, hids, grads, mine[4], mine[5] if first else None)
        if final:
            rights, strips = ([g[i] for g in groups[2::2]] + [mine[i]] for i in (3, 4))
            mirrors = [g[5] if len(g) > 5 else None for g in groups[2::2] + [mine]]
            finish(every, inns, hids, grads, rights, strips, mirrors, own, out_ref, tail[-1])

    vmem = pl.BlockSpec(memory_space=pltpu.VMEM)
    if final:
        out_shape = jax.ShapeDtypeStruct((own, 2 * width), jnp.float32)
        out_specs = vmem
        scratch = [pltpu.VMEM(*m) for m in made]
        scratch.append(pltpu.VMEM((count * rays, LANES), jnp.float32))
    else:
        out_shape = [jax.ShapeDtypeStruct(*m) for m in made]
        out_specs = [vmem] * len(made)
        scratch = []
    flops = 6 * rays * width * units + 4 * width * (last * last - first * first) * BLOCK * BLOCK
    return pl.pallas_call(
        kernel,
        out_shape=out_shape,
        in_specs=[vmem] * len(operands),
        out_specs=out_specs,
        scratch_shapes=scratch,
        cost_estimate=pl.CostEstimate(
            flops=flops, transcendentals=4 * rays * units, bytes_accessed=8 * rays * width
        ),
        compiler_params=pltpu.CompilerParams(vmem_limit_bytes=VMEM_BYTES),
    )(*operands)


def split3(value):
    high = value.astype(jnp.bfloat16).astype(jnp.float32)
    rest = value - high
    middle = rest.astype(jnp.bfloat16).astype(jnp.float32)
    return high, middle, rest - middle


def table(target, counts, views):
    rays = target.shape[0]

    def kernel(target_ref, counts_ref, views_ref, out_ref):
        rows = [ray_weight(counts_ref[...], views_ref[...]), target_ref[...]]
        rows.append(jnp.zeros((8 - len(rows), rays), jnp.float32))
        out_ref[:, 0:rays] = jnp.concatenate(rows, axis=0)
        out_ref[:, rays:LANES] = jnp.zeros((8, LANES - rays), jnp.float32)

    vmem = pl.BlockSpec(memory_space=pltpu.VMEM)
    return pl.pallas_call(
        kernel,
        out_shape=jax.ShapeDtypeStruct((8, LANES), jnp.float32),
        in_specs=[vmem] * 3,
        out_specs=vmem,
        compiler_params=pltpu.CompilerParams(vmem_limit_bytes=2**20),
        name="table",
    )(target[None, :], counts[None, :], views[None, :])


def join(pieces, tables):
    count = len(pieces)
    rays, width = pieces[0].shape

    def kernel(*refs):
        out_ref = refs[-1]
        for k in range(count):
            rows = slice(k * rays, (k + 1) * rays)
            out_ref[rows, 0:width] = refs[k][...]
            values = refs[count + k][...]
            terms = [*split3(values[0:1, :]), *split3(values[1:2, :])]
            terms.append(jnp.zeros((LANES - len(terms), LANES), jnp.float32))
            square = jnp.concatenate(terms, axis=0).T
            out_ref[rows, width : width + LANES] = square[0:rays, :].astype(jnp.bfloat16)

    vmem = pl.BlockSpec(memory_space=pltpu.VMEM)
    return pl.pallas_call(
        kernel,
        out_shape=jax.ShapeDtypeStruct((count * rays, width + LANES), pieces[0].dtype),
        in_specs=[vmem] * (2 * count),
        out_specs=vmem,
        compiler_params=pltpu.CompilerParams(vmem_limit_bytes=2**21),
        name="join",
    )(*pieces, *tables)


def load(first_weight, second_weight):
    def kernel(a_ref, b_ref, a_out, b_out, sems):
        copies = [
            pltpu.make_async_copy(a_ref, a_out, sems.at[0]),
            pltpu.make_async_copy(b_ref, b_out, sems.at[1]),
        ]
        for copy in copies:
            copy.start()
        for copy in copies:
            copy.wait()

    both = [jax.ShapeDtypeStruct(a.shape, a.dtype) for a in (first_weight, second_weight)]
    return pl.pallas_call(
        kernel,
        out_shape=both,
        in_specs=[pl.BlockSpec(memory_space=pltpu.HBM)] * 2,
        out_specs=[pl.BlockSpec(memory_space=pltpu.VMEM)] * 2,
        scratch_shapes=[pltpu.SemaphoreType.DMA((2,))],
        compiler_params=pltpu.CompilerParams(vmem_limit_bytes=6 * 2**20),
        name="load",
    )(first_weight, second_weight)


def gathered(inputs, first_weight, second_weight, readout, target, counts, views):
    n_row, n_col = lax.axis_size("row"), lax.axis_size("col")
    line = n_row // 4
    _, width = inputs.shape

    def swap(value, moves):
        pairs = []
        for r in range(n_row):
            for c in range(n_col):
                row_bits, col_bits = moves[r % 2]
                pairs.append((r * n_col + c, (r ^ row_bits) * n_col + (c ^ col_bits)))
        return lax.ppermute(value, ("row", "col"), pairs)

    units = [inputs] + [swap(inputs, ((4 * k, 0),) * 2) for k in range(1, line)]
    own_table = table(target, counts, views)
    tables = [own_table]
    tables += [swap(own_table, ((4 * k, 0),) * 2) for k in range(1, line)]
    first_weight, second_weight = load(first_weight, second_weight)
    halves = [join(units, tables)]
    straight, crossed = ((0, 1), (2, 0)), ((2, 0), (0, 1))
    halves.append(swap(halves[0], straight))
    halves.append(swap(halves[0], crossed))
    halves.append(swap(halves[1], crossed))
    ro = readout.astype(jnp.float32)[None, :]
    before = []
    for k, half in enumerate(halves):
        pays = [half, swap(half, ((1, 0),) * 2)]
        got = stage(
            k, len(halves), pays, first_weight, second_weight, ro, before, width // (n_row * n_col)
        )
        before.append({"pays": pays, "made": got})
    return got


def solution(mesh):
    in_specs = (
        P(("row", "col"), None),
        P(),
        P(),
        P(),
        P(("row", "col")),
        P(("row", "col")),
        P(("row", "col")),
    )
    out_specs = P(("row", "col"), None)
    n_row, n_col = mesh.shape["row"], mesh.shape["col"]

    def body(inputs, *rest):
        rays = inputs.shape[0] * n_row * n_col
        chunk = rays // 4
        width = inputs.shape[1]
        own = width // (n_row * n_col)
        held = 4 * rays * rays + 8 * rays * width
        fits = held <= VMEM_BYTES and n_col == 2 and n_row in (4, 8, 16, 32)
        fits = fits and chunk % LANES == 0 and chunk >= BLOCK and rays % BLOCK == 0
        fits = fits and width % LANES == 0 and own * n_row * n_col == width
        fits = fits and own % 8 == 0 and LANES % own == 0 and 3 * own <= LANES
        if not fits:
            return shards(inputs, *rest)
        return gathered(inputs, *rest)

    return jax.shard_map(body, mesh=mesh, in_specs=in_specs, out_specs=out_specs, check_vma=False)
```

profile of v0, /device:TPU:0, one launch (start us, length us, event | category | flops | bytes accessed | tf_op | source)
XLA Modules:
  0.0 68.2 jit_solution(3937767708511577549)
XLA Ops:
  0.0 4.1 %collective-permute-start.1 = (bf16[48,1024]{1,0:T(8,128)(2,1)}, bf16[48,1024]{1,0:T(8,128)(2,1)S(1)}, u32[]{:S(2)}, u32[]{:S(2)}) collective-permute-start(bf16[48,1024]{1,0:T(8,128)(2,1)} %refs_0_.1), channel_id=1, source_target_pairs={{0,16},{1,17},{2,18},{3,19},{4,20},{5,21},{6,22},{7,23},{8,24},{9,... | collective-permute-start | bytes 294920 | tf_op jit(solution)/shard_map/ppermute | solution.py:434
  4.1 1.6 %collective-permute-start = (bf16[48,1024]{1,0:T(8,128)(2,1)}, bf16[48,1024]{1,0:T(8,128)(2,1)S(1)}, u32[]{:S(2)}, u32[]{:S(2)}) collective-permute-start(bf16[48,1024]{1,0:T(8,128)(2,1)} %refs_0_.1), channel_id=1, source_target_pairs={{0,8},{1,9},{2,10},{3,11},{4,12},{5,13},{6,14},{7,15},{8,0},{9,1},... | collective-permute-start | bytes 294920 | tf_op jit(solution)/shard_map/ppermute | solution.py:434
  5.6 0.7 copy-done.3
  6.3 0.7 copy-done.4
  7.0 0.7 copy-done.5
  7.7 3.9 %collective-permute-start.5 = (f32[8,128]{1,0:T(8,128)S(1)}, f32[8,128]{1,0:T(8,128)S(1)}, u32[]{:S(2)}, u32[]{:S(2)}) collective-permute-start(f32[8,128]{1,0:T(8,128)S(1)} %table.1.refs_4_), channel_id=1, source_target_pairs={{0,24},{1,25},{2,26},{3,27},{4,28},{5,29},{6,30},{7,31},{8,16},{9,... | collective-permute-start | bytes 12296 | tf_op jit(solution)/shard_map/ppermute | solution.py:434
  11.6 1.7 %collective-permute-done.5.refs_7_ = f32[8,128]{1,0:T(8,128)S(1)} collective-permute-done((f32[8,128]{1,0:T(8,128)S(1)}, f32[8,128]{1,0:T(8,128)S(1)}, u32[]{:S(2)}, u32[]{:S(2)}) %collective-permute-start.5) | collective-permute-done | bytes 4128 | tf_op jit(solution)/shard_map/ppermute | solution.py:434
  13.2 1.2 %collective-permute-start.3 = (f32[8,128]{1,0:T(8,128)S(1)}, f32[8,128]{1,0:T(8,128)S(1)}, u32[]{:S(2)}, u32[]{:S(2)}) collective-permute-start(f32[8,128]{1,0:T(8,128)S(1)} %table.1.refs_4_), channel_id=1, source_target_pairs={{0,8},{1,9},{2,10},{3,11},{4,12},{5,13},{6,14},{7,15},{8,0},{9,1},... | collective-permute-start | bytes 12296 | tf_op jit(solution)/shard_map/ppermute | solution.py:434
  14.4 1.6 %collective-permute-done.4.refs_6_ = f32[8,128]{1,0:T(8,128)S(1)} collective-permute-done((f32[8,128]{1,0:T(8,128)S(1)}, f32[8,128]{1,0:T(8,128)S(1)}, u32[]{:S(2)}, u32[]{:S(2)}) %collective-permute-start.4) | collective-permute-done | bytes 4128 | tf_op jit(solution)/shard_map/ppermute | solution.py:434
  16.1 0.8 %collective-permute-done.3.refs_5_ = f32[8,128]{1,0:T(8,128)S(1)} collective-permute-done((f32[8,128]{1,0:T(8,128)S(1)}, f32[8,128]{1,0:T(8,128)S(1)}, u32[]{:S(2)}, u32[]{:S(2)}) %collective-permute-start.3) | collective-permute-done | bytes 4128 | tf_op jit(solution)/shard_map/ppermute | solution.py:434
  16.8 0.0 collective-permute-done.1.refs_2_
  16.8 0.0 collective-permute-done.refs_1_
  16.8 0.0 collective-permute-done.2.refs_3_
  16.9 0.0 copy-start.2
  16.9 0.9 %copy-done.2 = bf16[48,1024]{1,0:T(8,128)(2,1)S(1)} copy-done((bf16[48,1024]{1,0:T(8,128)(2,1)S(1)}, bf16[48,1024]{1,0:T(8,128)(2,1)}, u32[]{:S(2)}) %copy-start.2) | copy-done | bytes 98328
  17.8 0.1 join.1.refs_0_.refs_5_
  17.9 1.8 %collective-permute-start.6 = (bf16[192,1152]{1,0:T(8,128)(2,1)S(1)}, bf16[192,1152]{1,0:T(8,128)(2,1)S(1)}, u32[]{:S(2)}, u32[]{:S(2)}) collective-permute-start(bf16[192,1152]{1,0:T(8,128)(2,1)S(1)} %join.1.refs_0_.refs_5_), channel_id=1, source_target_pairs={{0,1},{1,0},{2,6},{3,7},{4,5},{5,4},{6,2},{7,3},{8,9},{9,8},{10,14... | collective-permute-start | bytes 1327112 | tf_op jit(solution)/shard_map/ppermute | solution.py:434
  19.6 1.5 %collective-permute-start.11 = (bf16[192,1152]{1,0:T(8,128)(2,1)S(1)}, bf16[192,1152]{1,0:T(8,128)(2,1)S(1)}, u32[]{:S(2)}, u32[]{:S(2)}) collective-permute-start(bf16[192,1152]{1,0:T(8,128)(2,1)S(1)} %join.1.refs_0_.refs_5_), channel_id=1, source_target_pairs={{0,4},{1,5},{2,3},{3,2},{4,0},{5,1},{6,7},{7,6},{8,12},{9,13},{10,... | collective-permute-start | bytes 1327112 | tf_op jit(solution)/shard_map/ppermute | solution.py:434
  21.2 0.0 collective-permute-start.9
  21.2 9.8 %collective-permute-done.6.refs_0_.refs_10_.refs_12_ = bf16[192,1152]{1,0:T(8,128)(2,1)S(1)} collective-permute-done((bf16[192,1152]{1,0:T(8,128)(2,1)S(1)}, bf16[192,1152]{1,0:T(8,128)(2,1)S(1)}, u32[]{:S(2)}, u32[]{:S(2)}) %collective-permute-start.6) | collective-permute-done | bytes 442400 | tf_op jit(solution)/shard_map/ppermute | solution.py:434
  31.0 0.3 collective-permute-start.7
  31.2 0.0 collective-permute-start.10
  31.2 0.7 %broadcast_in_dim.19 = f32[1024]{0:T(1024)S(1)} convert(bf16[1024]{0:T(1024)(128)(2,1)} %param.10) | non-fusion elementwise | flops 1024 | bytes 6144 | tf_op jit(solution)/shard_map/broadcast_in_dim | solution.py:446
  31.9 1.6 %copy-done = bf16[1024,1024]{1,0:T(8,128)(2,1)S(1)} copy-done((bf16[1024,1024]{1,0:T(8,128)(2,1)S(1)}, bf16[1024,1024]{1,0:T(8,128)(2,1)}, u32[]{:S(2)}) %copy-start) | copy-done | bytes 2097176
  33.5 1.6 %copy-done.1 = bf16[1024,1024]{1,0:T(8,128)(2,1)S(1)} copy-done((bf16[1024,1024]{1,0:T(8,128)(2,1)S(1)}, bf16[1024,1024]{1,0:T(8,128)(2,1)}, u32[]{:S(2)}) %copy-start.1) | copy-done | bytes 2097176
  35.1 0.3 load.1
  35.4 0.6 collective-permute-start.12
  36.0 3.7 %shard_map.73 = (bf16[384,1024]{1,0:T(8,128)(2,1)S(1)}, bf16[384,1024]{1,0:T(8,128)(2,1)S(1)}, bf16[384,1024]{1,0:T(8,128)(2,1)S(1)}, f32[384,128]{1,0:T(8,128)S(1)}, f32[256,256]{1,0:T(8,128)S(1)}) custom-call(bf16[192,1152]{1,0:T(8,128)(2,1)S(1)} %join.1.refs_0_.refs_5_, bf16[192,1152]{1,0:T(8,128)(2,1)S(1)} %collective-permute-done.9.refs_1_.refs_6_, ...), custom_call_target="tpu_custom_call" | custom-call | flops 2684354560 | bytes 3145728 | tf_op jit(solution)/shard_map/pallas_call | solution.py:334
  39.7 0.1 collective-permute-start.8
  39.8 5.9 %shard_map.74 = (bf16[384,1024]{1,0:T(8,128)(2,1)S(1)}, bf16[384,1024]{1,0:T(8,128)(2,1)S(1)}, bf16[384,1024]{1,0:T(8,128)(2,1)S(1)}, f32[384,128]{1,0:T(8,128)S...) custom-call(bf16[192,1152]{1,0:T(8,128)(2,1)S(1)} %collective-permute-done.6.refs_0_.refs_10_.refs_12_, ...), custom_call_target="tpu_custom_call" | custom-call | flops 4563402752 | bytes 3145728 | tf_op jit(solution)/shard_map/pallas_call | solution.py:334
  45.8 5.6 %shard_map.75 = (bf16[384,1024]{1,0:T(8,128)(2,1)S(1)}, bf16[384,1024]{1,0:T(8,128)(2,1)S(1)}, bf16[384,1024]{1,0:T(8,128)(2,1)S(1)}, f32[384,128]{1,0:T(8,128)S...) custom-call(bf16[192,1152]{1,0:T(8,128)(2,1)S(1)} %collective-permute-done.11.refs_0_.refs_20_, ...), custom_call_target="tpu_custom_call" | custom-call | flops 4294967296 | bytes 3145728 | tf_op jit(solution)/shard_map/pallas_call | solution.py:334
  51.3 16.9 %shard_map.76 = f32[32,2048]{1,0:T(8,128)} custom-call(bf16[192,1152]{1,0:T(8,128)(2,1)S(1)} %collective-permute-done.7.refs_0_, bf16[192,1152]{1,0:T(8,128)(2,1)S(1)} %collective-permute-done.8.refs_1_, bf16[1024,1024]{1,0:T(8,128)(2,1)S(1)} %get-tuple-element.24.refs_2_, bf16[1024,1024]{1,0:T(8,128)(2,1)S(1)} %get-tuple-element.25.refs_3_, ...), custom_call_target="tpu_custom_call" | custom-call | flops 7784628224 | bytes 3145728 | tf_op jit(solution)/shard_map/pallas_call | solution.py:334
  (14 shorter events, 0.1 us)
Async XLA Ops:
  0.0 16.8 %collective-permute-start.1 = (bf16[48,1024]{1,0:T(8,128)(2,1)}, bf16[48,1024]{1,0:T(8,128)(2,1)S(1)}, u32[]{:S(2)}, u32[]{:S(2)}) collective-permute-start(bf16[48,1024]{1,0:T(8,128)(2,1)} %refs_0_.1), channel_id=1, source_target_pairs={{0,16},{1,17},{2,18},{3,19},{4,20},{5,21},{6,22},{7,23},{8,24},{9,... | collective-permute-start | bytes 294920 | tf_op jit(solution)/shard_map/ppermute | solution.py:434
  4.1 12.8 %collective-permute-start = (bf16[48,1024]{1,0:T(8,128)(2,1)}, bf16[48,1024]{1,0:T(8,128)(2,1)S(1)}, u32[]{:S(2)}, u32[]{:S(2)}) collective-permute-start(bf16[48,1024]{1,0:T(8,128)(2,1)} %refs_0_.1), channel_id=1, source_target_pairs={{0,8},{1,9},{2,10},{3,11},{4,12},{5,13},{6,14},{7,15},{8,0},{9,1},... | collective-permute-start | bytes 294920 | tf_op jit(solution)/shard_map/ppermute | solution.py:434
  5.6 11.2 %collective-permute-start.2 = (bf16[48,1024]{1,0:T(8,128)(2,1)}, bf16[48,1024]{1,0:T(8,128)(2,1)S(1)}, u32[]{:S(2)}, u32[]{:S(2)}) collective-permute-start(bf16[48,1024]{1,0:T(8,128)(2,1)} %refs_0_.1), channel_id=1, source_target_pairs={{0,24},{1,25},{2,26},{3,27},{4,28},{5,29},{6,30},{7,31},{8,16},{9,... | collective-permute-start | bytes 294920 | tf_op jit(solution)/shard_map/ppermute | solution.py:434
  5.6 0.7 copy-start.3
  6.3 0.7 copy-start.4
  7.0 0.7 copy-start.5
  7.7 5.6 %collective-permute-start.5 = (f32[8,128]{1,0:T(8,128)S(1)}, f32[8,128]{1,0:T(8,128)S(1)}, u32[]{:S(2)}, u32[]{:S(2)}) collective-permute-start(f32[8,128]{1,0:T(8,128)S(1)} %table.1.refs_4_), channel_id=1, source_target_pairs={{0,24},{1,25},{2,26},{3,27},{4,28},{5,29},{6,30},{7,31},{8,16},{9,... | collective-permute-start | bytes 12296 | tf_op jit(solution)/shard_map/ppermute | solution.py:434
  11.5 4.5 %collective-permute-start.4 = (f32[8,128]{1,0:T(8,128)S(1)}, f32[8,128]{1,0:T(8,128)S(1)}, u32[]{:S(2)}, u32[]{:S(2)}) collective-permute-start(f32[8,128]{1,0:T(8,128)S(1)} %table.1.refs_4_), channel_id=1, source_target_pairs={{0,16},{1,17},{2,18},{3,19},{4,20},{5,21},{6,22},{7,23},{8,24},{9,... | collective-permute-start | bytes 12296 | tf_op jit(solution)/shard_map/ppermute | solution.py:434
  13.2 3.6 %collective-permute-start.3 = (f32[8,128]{1,0:T(8,128)S(1)}, f32[8,128]{1,0:T(8,128)S(1)}, u32[]{:S(2)}, u32[]{:S(2)}) collective-permute-start(f32[8,128]{1,0:T(8,128)S(1)} %table.1.refs_4_), channel_id=1, source_target_pairs={{0,8},{1,9},{2,10},{3,11},{4,12},{5,13},{6,14},{7,15},{8,0},{9,1},... | collective-permute-start | bytes 12296 | tf_op jit(solution)/shard_map/ppermute | solution.py:434
  16.9 0.9 %copy-start.2 = (bf16[48,1024]{1,0:T(8,128)(2,1)S(1)}, bf16[48,1024]{1,0:T(8,128)(2,1)}, u32[]{:S(2)}) copy-start(bf16[48,1024]{1,0:T(8,128)(2,1)} %refs_0_.1) | copy-start | bytes 294916
  17.9 13.1 %collective-permute-start.6 = (bf16[192,1152]{1,0:T(8,128)(2,1)S(1)}, bf16[192,1152]{1,0:T(8,128)(2,1)S(1)}, u32[]{:S(2)}, u32[]{:S(2)}) collective-permute-start(bf16[192,1152]{1,0:T(8,128)(2,1)S(1)} %join.1.refs_0_.refs_5_), channel_id=1, source_target_pairs={{0,1},{1,0},{2,6},{3,7},{4,5},{5,4},{6,2},{7,3},{8,9},{9,8},{10,14... | collective-permute-start | bytes 1327112 | tf_op jit(solution)/shard_map/ppermute | solution.py:434
  19.6 15.8 %collective-permute-start.11 = (bf16[192,1152]{1,0:T(8,128)(2,1)S(1)}, bf16[192,1152]{1,0:T(8,128)(2,1)S(1)}, u32[]{:S(2)}, u32[]{:S(2)}) collective-permute-start(bf16[192,1152]{1,0:T(8,128)(2,1)S(1)} %join.1.refs_0_.refs_5_), channel_id=1, source_target_pairs={{0,4},{1,5},{2,3},{3,2},{4,0},{5,1},{6,7},{7,6},{8,12},{9,13},{10,... | collective-permute-start | bytes 1327112 | tf_op jit(solution)/shard_map/ppermute | solution.py:434
  21.2 14.9 %collective-permute-start.9 = (bf16[192,1152]{1,0:T(8,128)(2,1)S(1)}, bf16[192,1152]{1,0:T(8,128)(2,1)S(1)}, u32[]{:S(2)}, u32[]{:S(2)}) collective-permute-start(bf16[192,1152]{1,0:T(8,128)(2,1)S(1)} %join.1.refs_0_.refs_5_), channel_id=1, source_target_pairs={{0,2},{1,3},{2,0},{3,1},{4,6},{5,7},{6,4},{7,5},{8,10},{9,11},{10,... | collective-permute-start | bytes 1327112 | tf_op jit(solution)/shard_map/ppermute | solution.py:434
  31.0 8.8 %collective-permute-start.7 = (bf16[192,1152]{1,0:T(8,128)(2,1)S(1)}, bf16[192,1152]{1,0:T(8,128)(2,1)S(1)}, u32[]{:S(2)}, u32[]{:S(2)}) collective-permute-start(bf16[192,1152]{1,0:T(8,128)(2,1)S(1)} %collective-permute-done.6.refs_0_.refs_10_.refs_12_), channel_id=1, source_target_pairs={{0,4},{1,5},{2,3},{3,2},{4,0},{5,1},{6,7},{7,6},{8,12},{9,13},{10,... | collective-permute-start | bytes 1327112 | tf_op jit(solution)/shard_map/ppermute | solution.py:434
  31.2 8.6 %collective-permute-start.10 = (bf16[192,1152]{1,0:T(8,128)(2,1)S(1)}, bf16[192,1152]{1,0:T(8,128)(2,1)S(1)}, u32[]{:S(2)}, u32[]{:S(2)}) collective-permute-start(bf16[192,1152]{1,0:T(8,128)(2,1)S(1)} %collective-permute-done.6.refs_0_.refs_10_.refs_12_), channel_id=1, source_target_pairs={{0,2},{1,3},{2,0},{3,1},{4,6},{5,7},{6,4},{7,5},{8,10},{9,11},{10,... | collective-permute-start | bytes 1327112 | tf_op jit(solution)/shard_map/ppermute | solution.py:434
  31.9 1.6 %copy-start = (bf16[1024,1024]{1,0:T(8,128)(2,1)S(1)}, bf16[1024,1024]{1,0:T(8,128)(2,1)}, u32[]{:S(2)}) copy-start(bf16[1024,1024]{1,0:T(8,128)(2,1)} %a_ref.1) | copy-start | bytes 6291460
  33.5 1.6 %copy-start.1 = (bf16[1024,1024]{1,0:T(8,128)(2,1)S(1)}, bf16[1024,1024]{1,0:T(8,128)(2,1)}, u32[]{:S(2)}) copy-start(bf16[1024,1024]{1,0:T(8,128)(2,1)} %b_ref.1) | copy-start | bytes 6291460
  35.4 10.3 %collective-permute-start.12 = (bf16[192,1152]{1,0:T(8,128)(2,1)S(1)}, bf16[192,1152]{1,0:T(8,128)(2,1)S(1)}, u32[]{:S(2)}, u32[]{:S(2)}) collective-permute-start(bf16[192,1152]{1,0:T(8,128)(2,1)S(1)} %collective-permute-done.11.refs_0_.refs_20_), channel_id=1, source_target_pairs={{0,2},{1,3},{2,0},{3,1},{4,6},{5,7},{6,4},{7,5},{8,10},{9,11},{10,... | collective-permute-start | bytes 1327112 | tf_op jit(solution)/shard_map/ppermute | solution.py:434
  39.7 11.6 %collective-permute-start.8 = (bf16[192,1152]{1,0:T(8,128)(2,1)S(1)}, bf16[192,1152]{1,0:T(8,128)(2,1)S(1)}, u32[]{:S(2)}, u32[]{:S(2)}) collective-permute-start(bf16[192,1152]{1,0:T(8,128)(2,1)S(1)} %collective-permute-done.7.refs_0_), channel_id=1, source_target_pairs={{0,2},{1,3},{2,0},{3,1},{4,6},{5,7},{6,4},{7,5},{8,10},{9,11},{10,... | collective-permute-start | bytes 1327112 | tf_op jit(solution)/shard_map/ppermute | solution.py:434
where the time goes:
time: 68.5 us; the launch traced here: 68.2 us
  Pallas kernels  32.5 us (47%)
  starting transfers between devices  14.9 us (22%)
  waiting for transfers between devices  13.9 us (20%)
  local copies, waits for them, and re-layouts  6.03 us (9%)
    pallas_call x4, Pallas kernels, stage(): pl.pallas_call(kernel, out_shape=out_shape, in_specs=[vmem] * len(operand...  32.1 us
    ppermute x13, starting transfers between devices, swap(): return lax.ppermute(value, ('row', 'col'), pairs)  14.9 us
    ppermute x13, waiting for transfers between devices, swap(): return lax.ppermute(value, ('row', 'col'), pairs)  13.9 us
    unnamed x12, local copies, waits for them, and re-layouts  6.03 us
  transfers between devices with their start and end apart: 13, of which 4 were waited for; matrix products, arithmetic and copies ran while one was open for 1% of the time, Pallas kernels for 23%

commit v1 on v0

--- a/solution.py
+++ b/solution.py
@@ -221,7 +221,6 @@
             pieces[k] = a if pieces[k] is None else pieces[k] + a
 
     def apply(row):
-        to_columns(row)
         pieces, offset = [None] * tiles, 0
         for strip, mirror in zip(strips, mirrors):
             sweep(strip, offset, pieces, 0)
@@ -245,7 +244,13 @@
     answer = jnp.zeros_like(right)
     residual, direction = right, right
     norm_now = dot(right, right)
+    offset = 0
+    for ref in rights:
+        col_ref[offset : offset + ref.shape[0], :] = ref[...]
+        offset += ref.shape[0]
     for step in range(ITERS):
+        if step:
+            to_columns(direction)
         image = apply(direction)
         alpha = norm_now / dot(direction, image)
         answer = answer + alpha * direction
@@ -351,46 +356,34 @@
     return high, middle, rest - middle
 
 
-def table(target, counts, views):
-    rays = target.shape[0]
-
-    def kernel(target_ref, counts_ref, views_ref, out_ref):
-        rows = [ray_weight(counts_ref[...], views_ref[...]), target_ref[...]]
-        rows.append(jnp.zeros((8 - len(rows), rays), jnp.float32))
-        out_ref[:, 0:rays] = jnp.concatenate(rows, axis=0)
-        out_ref[:, rays:LANES] = jnp.zeros((8, LANES - rays), jnp.float32)
+def place_terms(out_ref, start, values, width):
+    rays = values.shape[1]
+    terms = [*split3(values[0:1, :]), *split3(values[1:2, :])]
+    terms.append(jnp.zeros((LANES - len(terms), rays), jnp.float32))
+    square = jnp.concatenate(terms, axis=0)
+    square = jnp.concatenate([square, jnp.zeros((LANES, LANES - rays), jnp.float32)], axis=1).T
+    out_ref[start : start + rays, width : width + LANES] = square[0:rays].astype(jnp.bfloat16)
+
+
+def join(pieces, tables=()):
+    count = len(pieces)
+    rows, width = sum(a.shape[0] for a in pieces), pieces[0].shape[1]
+
+    def kernel(*refs):
+        out_ref, start = refs[-1], 0
+        for k in range(count):
+            stop = start + refs[k].shape[0]
+            out_ref[start:stop, 0:width] = refs[k][...]
+            if tables:
+                place_terms(out_ref, start, refs[count + k][...], width)
+            start = stop
 
     vmem = pl.BlockSpec(memory_space=pltpu.VMEM)
+    wide = width + LANES if tables else width
     return pl.pallas_call(
         kernel,
-        out_shape=jax.ShapeDtypeStruct((8, LANES), jnp.float32),
-        in_specs=[vmem] * 3,
-        out_specs=vmem,
-        compiler_params=pltpu.CompilerParams(vmem_limit_bytes=2**20),
-        name="table",
-    )(target[None, :], counts[None, :], views[None, :])
-
-
-def join(pieces, tables):
-    count = len(pieces)
-    rays, width = pieces[0].shape
-
-    def kernel(*refs):
-        out_ref = refs[-1]
-        for k in range(count):
-            rows = slice(k * rays, (k + 1) * rays)
-            out_ref[rows, 0:width] = refs[k][...]
-            values = refs[count + k][...]
-            terms = [*split3(values[0:1, :]), *split3(values[1:2, :])]
-            terms.append(jnp.zeros((LANES - len(terms), LANES), jnp.float32))
-            square = jnp.concatenate(terms, axis=0).T
-            out_ref[rows, width : width + LANES] = square[0:rays, :].astype(jnp.bfloat16)
-
-    vmem = pl.BlockSpec(memory_space=pltpu.VMEM)
-    return pl.pallas_call(
-        kernel,
-        out_shape=jax.ShapeDtypeStruct((count * rays, width + LANES), pieces[0].dtype),
-        in_specs=[vmem] * (2 * count),
+        out_shape=jax.ShapeDtypeStruct((rows, wide), pieces[0].dtype),
+        in_specs=[vmem] * (count + len(tables)),
         out_specs=vmem,
         compiler_params=pltpu.CompilerParams(vmem_limit_bytes=2**21),
         name="join",
@@ -423,7 +416,7 @@
 def gathered(inputs, first_weight, second_weight, readout, target, counts, views):
     n_row, n_col = lax.axis_size("row"), lax.axis_size("col")
     line = n_row // 4
-    _, width = inputs.shape
+    rays, width = inputs.shape
 
     def swap(value, moves):
         pairs = []
@@ -433,16 +426,25 @@
                 pairs.append((r * n_col + c, (r ^ row_bits) * n_col + (c ^ col_bits)))
         return lax.ppermute(value, ("row", "col"), pairs)
 
-    units = [inputs] + [swap(inputs, ((4 * k, 0),) * 2) for k in range(1, line)]
-    own_table = table(target, counts, views)
-    tables = [own_table]
-    tables += [swap(own_table, ((4 * k, 0),) * 2) for k in range(1, line)]
+    first_row = lax.broadcasted_iota(jnp.int32, (2, rays), 0) == 0
+    table = jnp.where(first_row, ray_weight(counts, views)[None, :], target[None, :])
+    units, tables = [inputs], [table]
+    for k in range(1, line):
+        units.append(swap(inputs, ((4 * k, 0),) * 2))
+        tables.append(swap(table, ((4 * k, 0),) * 2))
     first_weight, second_weight = load(first_weight, second_weight)
-    halves = [join(units, tables)]
     straight, crossed = ((0, 1), (2, 0)), ((2, 0), (0, 1))
-    halves.append(swap(halves[0], straight))
-    halves.append(swap(halves[0], crossed))
-    halves.append(swap(halves[1], crossed))
+    base, one, two, three = [], [], [], []
+    for k in range(2):
+        some = slice(k * line // 2, (k + 1) * line // 2)
+        base.append(join(units[some], tables[some]))
+        one.append(swap(base[k], straight))
+        two.append(swap(base[k], crossed))
+        three.append(swap(one[k], crossed))
+    parts = ((base[0], one[0]), (base[1], two[0]), (three[0], one[1]), (three[1], two[1]))
+    halves = []
+    for both in parts:
+        halves.append(join(both))
     ro = readout.astype(jnp.float32)[None, :]
     before = []
     for k, half in enumerate(halves):
@@ -473,7 +475,7 @@
         width = inputs.shape[1]
         own = width // (n_row * n_col)
         held = 4 * rays * rays + 8 * rays * width
-        fits = held <= VMEM_BYTES and n_col == 2 and n_row in (4, 8, 16, 32)
+        fits = held <= VMEM_BYTES and n_col == 2 and n_row in (8, 16, 32)
         fits = fits and chunk % LANES == 0 and chunk >= BLOCK and rays % BLOCK == 0
         fits = fits and width % LANES == 0 and own * n_row * n_col == width
         fits = fits and own % 8 == 0 and LANES % own == 0 and 3 * own <= LANES

time: 68.5 us -> 69.3 us (1.012)
  the two profiles are of different devices: /device:TPU:0 before, /device:TPU:1 now
where the time goes in v1:
time: 69.3 us; the launch traced here: 69.1 us
  Pallas kernels  32.6 us (47%)
  starting transfers between devices  17.5 us (25%)
  waiting for transfers between devices  14.9 us (22%)
  local copies, waits for them, and re-layouts  2.49 us (4%)
  other arithmetic  1.45 us (2%)
    pallas_call x4, Pallas kernels, stage(): pl.pallas_call(kernel, out_shape=out_shape, in_specs=[vmem] * len(operand...  32 us
    ppermute x16, starting transfers between devices, swap(): return lax.ppermute(value, ('row', 'col'), pairs)  17.5 us
    ppermute x16, waiting for transfers between devices, swap(): return lax.ppermute(value, ('row', 'col'), pairs)  14.9 us
    unnamed x8, local copies, waits for them, and re-layouts  2.49 us
  transfers between devices with their start and end apart: 16, of which 7 were waited for; matrix products, arithmetic and copies ran while one was open for 2% of the time, Pallas kernels for 23%

profile of v1, /device:TPU:1, one launch (start us, length us, event | category | flops | bytes accessed | tf_op | source)
XLA Modules:
  0.0 69.1 jit_solution(6797550865380973572)
XLA Ops:
  0.0 2.1 %collective-permute-start.8 = (bf16[48,1024]{1,0:T(8,128)(2,1)}, bf16[48,1024]{1,0:T(8,128)(2,1)S(1)}, u32[]{:S(2)}, u32[]{:S(2)}) collective-permute-start(bf16[48,1024]{1,0:T(8,128)(2,1)} %refs_0_.1), channel_id=1, source_target_pairs={{0,8},{1,9},{2,10},{3,11},{4,12},{5,13},{6,14},{7,15},{8,0},{9,1},... | collective-permute-start | bytes 294920 | tf_op jit(solution)/shard_map/ppermute | solution.py:427
  2.1 0.7 %add_multiply_fusion = f32[48]{0:T(128)S(1)} fusion(s32[48]{0:T(128)} %param.13, s32[48]{0:T(128)} %param.12), kind=kLoop, calls=%fused_computation.1 | loop fusion | flops 336 | bytes 576 | tf_op jit(solution)/shard_map/mul | solution.py:28
  2.8 0.7 %broadcast_select_fusion.refs_2_ = f32[2,48]{1,0:T(2,128)S(1)} fusion(pred[2]{0:T(512)(128)(4,1)S(1)} %iota_compare_fusion, f32[48]{0:T(128)} %param.11, f32[48]{0:T(128)S(1)} %add_multiply_fusion), kind=kLoop, calls=%fused_computation | loop fusion | flops 96 | bytes 770 | tf_op jit(solution)/shard_map/jit(_where)/select_n | solution.py:430
  3.6 0.2 collective-permute-start.9
  3.7 2.3 %collective-permute-done.9.refs_3_ = f32[2,48]{1,0:T(2,128)S(1)} collective-permute-done((f32[2,48]{1,0:T(2,128)S(1)}, f32[2,48]{1,0:T(2,128)S(1)}, u32[]{:S(2)}, u32[]{:S(2)}) %collective-permute-start.9) | collective-permute-done | bytes 416 | tf_op jit(solution)/shard_map/ppermute | solution.py:427
  6.0 0.9 %copy-done.2 = bf16[48,1024]{1,0:T(8,128)(2,1)S(1)} copy-done((bf16[48,1024]{1,0:T(8,128)(2,1)S(1)}, bf16[48,1024]{1,0:T(8,128)(2,1)}, u32[]{:S(2)}) %copy-start.2) | copy-done | bytes 98328
  6.9 0.1 join.8.refs_0_
  7.0 1.3 %collective-permute-start.10 = (bf16[96,1152]{1,0:T(8,128)(2,1)S(1)}, bf16[96,1152]{1,0:T(8,128)(2,1)S(1)}, u32[]{:S(2)}, u32[]{:S(2)}) collective-permute-start(bf16[96,1152]{1,0:T(8,128)(2,1)S(1)} %join.8.refs_0_), channel_id=1, source_target_pairs={{0,1},{1,0},{2,6},{3,7},{4,5},{5,4},{6,2},{7,3},{8,9},{9,8},{10,14... | collective-permute-start | bytes 663560 | tf_op jit(solution)/shard_map/ppermute | solution.py:427
  8.3 2.6 %collective-permute-start.1 = (bf16[48,1024]{1,0:T(8,128)(2,1)S(1)}, bf16[48,1024]{1,0:T(8,128)(2,1)S(1)}, u32[]{:S(2)}, u32[]{:S(2)}) collective-permute-start(bf16[48,1024]{1,0:T(8,128)(2,1)S(1)} %copy-done.2), channel_id=1, source_target_pairs={{0,24},{1,25},{2,26},{3,27},{4,28},{5,29},{6,30},{7,31},{8,16},{9,... | collective-permute-start | bytes 294920 | tf_op jit(solution)/shard_map/ppermute | solution.py:427
  10.9 2.1 %collective-permute-start.3 = (f32[2,48]{1,0:T(2,128)S(1)}, f32[2,48]{1,0:T(2,128)S(1)}, u32[]{:S(2)}, u32[]{:S(2)}) collective-permute-start(f32[2,48]{1,0:T(2,128)S(1)} %broadcast_select_fusion.refs_2_), channel_id=1, source_target_pairs={{0,24},{1,25},{2,26},{3,27},{4,28},{5,29},{6,30},{7,31},{8,16},{9,... | collective-permute-start | bytes 1160 | tf_op jit(solution)/shard_map/ppermute | solution.py:427
  13.0 0.3 collective-permute-start.2
  13.3 1.9 %collective-permute-done.3.refs_3_ = f32[2,48]{1,0:T(2,128)S(1)} collective-permute-done((f32[2,48]{1,0:T(2,128)S(1)}, f32[2,48]{1,0:T(2,128)S(1)}, u32[]{:S(2)}, u32[]{:S(2)}) %collective-permute-start.3) | collective-permute-done | bytes 416 | tf_op jit(solution)/shard_map/ppermute | solution.py:427
  15.1 4.4 %collective-permute-done.2.refs_2_ = f32[2,48]{1,0:T(2,128)S(1)} collective-permute-done((f32[2,48]{1,0:T(2,128)S(1)}, f32[2,48]{1,0:T(2,128)S(1)}, u32[]{:S(2)}, u32[]{:S(2)}) %collective-permute-start.2) | collective-permute-done | bytes 416 | tf_op jit(solution)/shard_map/ppermute | solution.py:427
  19.6 0.1 join.6.refs_0_
  19.8 2.8 %collective-permute-start.11 = (bf16[192,1152]{1,0:T(8,128)(2,1)S(1)}, bf16[192,1152]{1,0:T(8,128)(2,1)S(1)}, u32[]{:S(2)}, u32[]{:S(2)}) collective-permute-start(bf16[192,1152]{1,0:T(8,128)(2,1)S(1)} %join.9.refs_0_.refs_5_), channel_id=1, source_target_pairs={{0,2},{1,3},{2,0},{3,1},{4,6},{5,7},{6,4},{7,5},{8,10},{9,11},{10,... | collective-permute-start | bytes 1327112 | tf_op jit(solution)/shard_map/ppermute | solution.py:427
  22.6 0.5 collective-permute-start.12
  23.1 1.0 %collective-permute-start.6 = (bf16[96,1152]{1,0:T(8,128)(2,1)S(1)}, bf16[96,1152]{1,0:T(8,128)(2,1)S(1)}, u32[]{:S(2)}, u32[]{:S(2)}) collective-permute-start(bf16[96,1152]{1,0:T(8,128)(2,1)S(1)} %join.6.refs_0_), channel_id=1, source_target_pairs={{0,4},{1,5},{2,3},{3,2},{4,0},{5,1},{6,7},{7,6},{8,12},{9,13},{10,... | collective-permute-start | bytes 663560 | tf_op jit(solution)/shard_map/ppermute | solution.py:427
  24.0 0.8 %collective-permute-done.4.refs_1_ = bf16[96,1152]{1,0:T(8,128)(2,1)S(1)} collective-permute-done((bf16[96,1152]{1,0:T(8,128)(2,1)S(1)}, bf16[96,1152]{1,0:T(8,128)(2,1)S(1)}, u32[]{:S(2)}, u32[]{:S(2)}) %collective-permute-start.4) | collective-permute-done | bytes 221216 | tf_op jit(solution)/shard_map/ppermute | solution.py:427
  24.8 1.2 %collective-permute-start.5 = (bf16[96,1152]{1,0:T(8,128)(2,1)S(1)}, bf16[96,1152]{1,0:T(8,128)(2,1)S(1)}, u32[]{:S(2)}, u32[]{:S(2)}) collective-permute-start(bf16[96,1152]{1,0:T(8,128)(2,1)S(1)} %collective-permute-done.4.refs_1_), channel_id=1, source_target_pairs={{0,4},{1,5},{2,3},{3,2},{4,0},{5,1},{6,7},{7,6},{8,12},{9,13},{10,... | collective-permute-start | bytes 663560 | tf_op jit(solution)/shard_map/ppermute | solution.py:427
  26.0 0.2 collective-permute-start.14
  26.3 2.9 %collective-permute-done.12.refs_1_ = bf16[96,1152]{1,0:T(8,128)(2,1)S(1)} collective-permute-done((bf16[96,1152]{1,0:T(8,128)(2,1)S(1)}, bf16[96,1152]{1,0:T(8,128)(2,1)S(1)}, u32[]{:S(2)}, u32[]{:S(2)}) %collective-permute-start.12) | collective-permute-done | bytes 221216 | tf_op jit(solution)/shard_map/ppermute | solution.py:427
  29.2 1.6 %collective-permute-start.13 = (bf16[192,1152]{1,0:T(8,128)(2,1)S(1)}, bf16[192,1152]{1,0:T(8,128)(2,1)S(1)}, u32[]{:S(2)}, u32[]{:S(2)}) collective-permute-start(bf16[192,1152]{1,0:T(8,128)(2,1)S(1)} %join.10.refs_0_.refs_10_.refs_12_), channel_id=1, source_target_pairs={{0,2},{1,3},{2,0},{3,1},{4,6},{5,7},{6,4},{7,5},{8,10},{9,11},{10,... | collective-permute-start | bytes 1327112 | tf_op jit(solution)/shard_map/ppermute | solution.py:427
  30.8 1.6 %copy-done.1 = bf16[1024,1024]{1,0:T(8,128)(2,1)S(1)} copy-done((bf16[1024,1024]{1,0:T(8,128)(2,1)S(1)}, bf16[1024,1024]{1,0:T(8,128)(2,1)}, u32[]{:S(2)}) %copy-start.1) | copy-done | bytes 2097176
  32.4 0.3 load.1
  32.7 1.2 %collective-permute-done.5.refs_0_ = bf16[96,1152]{1,0:T(8,128)(2,1)S(1)} collective-permute-done((bf16[96,1152]{1,0:T(8,128)(2,1)S(1)}, bf16[96,1152]{1,0:T(8,128)(2,1)S(1)}, u32[]{:S(2)}, u32[]{:S(2)}) %collective-permute-start.5) | collective-permute-done | bytes 221216 | tf_op jit(solution)/shard_map/ppermute | solution.py:427
  33.9 0.8 %collective-permute-start.7 = (bf16[192,1152]{1,0:T(8,128)(2,1)S(1)}, bf16[192,1152]{1,0:T(8,128)(2,1)S(1)}, u32[]{:S(2)}, u32[]{:S(2)}) collective-permute-start(bf16[192,1152]{1,0:T(8,128)(2,1)S(1)} %join.7.refs_0_), channel_id=1, source_target_pairs={{0,2},{1,3},{2,0},{3,1},{4,6},{5,7},{6,4},{7,5},{8,10},{9,11},{10,... | collective-permute-start | bytes 1327112 | tf_op jit(solution)/shard_map/ppermute | solution.py:427
  34.7 1.6 %collective-permute-done.14.refs_0_ = bf16[96,1152]{1,0:T(8,128)(2,1)S(1)} collective-permute-done((bf16[96,1152]{1,0:T(8,128)(2,1)S(1)}, bf16[96,1152]{1,0:T(8,128)(2,1)S(1)}, u32[]{:S(2)}, u32[]{:S(2)}) %collective-permute-start.14) | collective-permute-done | bytes 221216 | tf_op jit(solution)/shard_map/ppermute | solution.py:427
  36.3 0.8 %collective-permute-start.15 = (bf16[192,1152]{1,0:T(8,128)(2,1)S(1)}, bf16[192,1152]{1,0:T(8,128)(2,1)S(1)}, u32[]{:S(2)}, u32[]{:S(2)}) collective-permute-start(bf16[192,1152]{1,0:T(8,128)(2,1)S(1)} %join.11.refs_0_.refs_20_), channel_id=1, source_target_pairs={{0,2},{1,3},{2,0},{3,1},{4,6},{5,7},{6,4},{7,5},{8,10},{9,11},{10,... | collective-permute-start | bytes 1327112 | tf_op jit(solution)/shard_map/ppermute | solution.py:427
  37.1 3.6 %shard_map.73 = (bf16[384,1024]{1,0:T(8,128)(2,1)S(1)}, bf16[384,1024]{1,0:T(8,128)(2,1)S(1)}, bf16[384,1024]{1,0:T(8,128)(2,1)S(1)}, f32[384,128]{1,0:T(8,128)S(1)}, f32[256,256]{1,0:T(8,128)S(1)}) custom-call(bf16[192,1152]{1,0:T(8,128)(2,1)S(1)} %join.9.refs_0_.refs_5_, bf16[192,1152]{1,0:T(8,128)(2,1)S(1)} %collective-permute-done.11.refs_1_.refs_6_, ...), custom_call_target="tpu_custom_call" | custom-call | flops 2684354560 | bytes 3145728 | tf_op jit(solution)/shard_map/pallas_call | solution.py:339
  40.7 5.9 %shard_map.74 = (bf16[384,1024]{1,0:T(8,128)(2,1)S(1)}, bf16[384,1024]{1,0:T(8,128)(2,1)S(1)}, bf16[384,1024]{1,0:T(8,128)(2,1)S(1)}, f32[384,128]{1,0:T(8,128)S...) custom-call(bf16[192,1152]{1,0:T(8,128)(2,1)S(1)} %join.10.refs_0_.refs_10_.refs_12_, ...), custom_call_target="tpu_custom_call" | custom-call | flops 4563402752 | bytes 3145728 | tf_op jit(solution)/shard_map/pallas_call | solution.py:339
  46.6 5.6 %shard_map.75 = (bf16[384,1024]{1,0:T(8,128)(2,1)S(1)}, bf16[384,1024]{1,0:T(8,128)(2,1)S(1)}, bf16[384,1024]{1,0:T(8,128)(2,1)S(1)}, f32[384,128]{1,0:T(8,128)S...) custom-call(bf16[192,1152]{1,0:T(8,128)(2,1)S(1)} %join.11.refs_0_.refs_20_, ...), custom_call_target="tpu_custom_call" | custom-call | flops 4294967296 | bytes 3145728 | tf_op jit(solution)/shard_map/pallas_call | solution.py:339
  52.3 16.8 %shard_map.76 = f32[32,2048]{1,0:T(8,128)} custom-call(bf16[192,1152]{1,0:T(8,128)(2,1)S(1)} %join.7.refs_0_, bf16[192,1152]{1,0:T(8,128)(2,1)S(1)} %collective-permute-done.7.refs_1_, bf16[1024,1024]{1,0:T(8,128)(2,1)S(1)} %get-tuple-element.24.refs_2_, bf16[1024,1024]{1,0:T(8,128)(2,1)S(1)} %get-tuple-element.25.refs_3_, f32[1,1024]{1,0:T(1,128)S(1)} %bitcast.4, ...), custom_call_target="tpu_custom_call" | custom-call | flops 7784628224 | bytes 3145728 | tf_op jit(solution)/shard_map/pallas_call | solution.py:339
  (23 shorter events, 0.2 us)
Async XLA Ops:
  0.0 30.8 %copy-start = (bf16[1024,1024]{1,0:T(8,128)(2,1)S(1)}, bf16[1024,1024]{1,0:T(8,128)(2,1)}, u32[]{:S(2)}) copy-start(bf16[1024,1024]{1,0:T(8,128)(2,1)} %a_ref.1) | copy-start | bytes 6291460
  0.0 6.0 %collective-permute-start.8 = (bf16[48,1024]{1,0:T(8,128)(2,1)}, bf16[48,1024]{1,0:T(8,128)(2,1)S(1)}, u32[]{:S(2)}, u32[]{:S(2)}) collective-permute-start(bf16[48,1024]{1,0:T(8,128)(2,1)} %refs_0_.1), channel_id=1, source_target_pairs={{0,8},{1,9},{2,10},{3,11},{4,12},{5,13},{6,14},{7,15},{8,0},{9,1},... | collective-permute-start | bytes 294920 | tf_op jit(solution)/shard_map/ppermute | solution.py:427
  3.6 2.4 %collective-permute-start.9 = (f32[2,48]{1,0:T(2,128)S(1)}, f32[2,48]{1,0:T(2,128)S(1)}, u32[]{:S(2)}, u32[]{:S(2)}) collective-permute-start(f32[2,48]{1,0:T(2,128)S(1)} %broadcast_select_fusion.refs_2_), channel_id=1, source_target_pairs={{0,8},{1,9},{2,10},{3,11},{4,12},{5,13},{6,14},{7,15},{8,0},{9,1},... | collective-permute-start | bytes 1160 | tf_op jit(solution)/shard_map/ppermute | solution.py:427
  6.0 0.9 %copy-start.2 = (bf16[48,1024]{1,0:T(8,128)(2,1)S(1)}, bf16[48,1024]{1,0:T(8,128)(2,1)}, u32[]{:S(2)}) copy-start(bf16[48,1024]{1,0:T(8,128)(2,1)} %refs_0_.1) | copy-start | bytes 294916
  6.9 23.9 %copy-start.3 = (bf16[1024]{0:T(1024)(128)(2,1)S(1)}, bf16[1024]{0:T(1024)(128)(2,1)}, u32[]{:S(2)}) copy-start(bf16[1024]{0:T(1024)(128)(2,1)} %param.10) | copy-start | bytes 6148
  7.0 12.8 %collective-permute-start.10 = (bf16[96,1152]{1,0:T(8,128)(2,1)S(1)}, bf16[96,1152]{1,0:T(8,128)(2,1)S(1)}, u32[]{:S(2)}, u32[]{:S(2)}) collective-permute-start(bf16[96,1152]{1,0:T(8,128)(2,1)S(1)} %join.8.refs_0_), channel_id=1, source_target_pairs={{0,1},{1,0},{2,6},{3,7},{4,5},{5,4},{6,2},{7,3},{8,9},{9,8},{10,14... | collective-permute-start | bytes 663560 | tf_op jit(solution)/shard_map/ppermute | solution.py:427
  8.3 11.3 %collective-permute-start.1 = (bf16[48,1024]{1,0:T(8,128)(2,1)S(1)}, bf16[48,1024]{1,0:T(8,128)(2,1)S(1)}, u32[]{:S(2)}, u32[]{:S(2)}) collective-permute-start(bf16[48,1024]{1,0:T(8,128)(2,1)S(1)} %copy-done.2), channel_id=1, source_target_pairs={{0,24},{1,25},{2,26},{3,27},{4,28},{5,29},{6,30},{7,31},{8,16},{9,... | collective-permute-start | bytes 294920 | tf_op jit(solution)/shard_map/ppermute | solution.py:427
  10.9 8.7 %collective-permute-start = (bf16[48,1024]{1,0:T(8,128)(2,1)S(1)}, bf16[48,1024]{1,0:T(8,128)(2,1)S(1)}, u32[]{:S(2)}, u32[]{:S(2)}) collective-permute-start(bf16[48,1024]{1,0:T(8,128)(2,1)S(1)} %copy-done.2), channel_id=1, source_target_pairs={{0,16},{1,17},{2,18},{3,19},{4,20},{5,21},{6,22},{7,23},{8,24},{9,... | collective-permute-start | bytes 294920 | tf_op jit(solution)/shard_map/ppermute | solution.py:427
  10.9 4.2 %collective-permute-start.3 = (f32[2,48]{1,0:T(2,128)S(1)}, f32[2,48]{1,0:T(2,128)S(1)}, u32[]{:S(2)}, u32[]{:S(2)}) collective-permute-start(f32[2,48]{1,0:T(2,128)S(1)} %broadcast_select_fusion.refs_2_), channel_id=1, source_target_pairs={{0,24},{1,25},{2,26},{3,27},{4,28},{5,29},{6,30},{7,31},{8,16},{9,... | collective-permute-start | bytes 1160 | tf_op jit(solution)/shard_map/ppermute | solution.py:427
  13.0 6.6 %collective-permute-start.2 = (f32[2,48]{1,0:T(2,128)S(1)}, f32[2,48]{1,0:T(2,128)S(1)}, u32[]{:S(2)}, u32[]{:S(2)}) collective-permute-start(f32[2,48]{1,0:T(2,128)S(1)} %broadcast_select_fusion.refs_2_), channel_id=1, source_target_pairs={{0,16},{1,17},{2,18},{3,19},{4,20},{5,21},{6,22},{7,23},{8,24},{9,... | collective-permute-start | bytes 1160 | tf_op jit(solution)/shard_map/ppermute | solution.py:427
  19.7 5.1 %collective-permute-start.4 = (bf16[96,1152]{1,0:T(8,128)(2,1)S(1)}, bf16[96,1152]{1,0:T(8,128)(2,1)S(1)}, u32[]{:S(2)}, u32[]{:S(2)}) collective-permute-start(bf16[96,1152]{1,0:T(8,128)(2,1)S(1)} %join.6.refs_0_), channel_id=1, source_target_pairs={{0,1},{1,0},{2,6},{3,7},{4,5},{5,4},{6,2},{7,3},{8,9},{9,8},{10,14... | collective-permute-start | bytes 663560 | tf_op jit(solution)/shard_map/ppermute | solution.py:427
  19.8 17.3 %collective-permute-start.11 = (bf16[192,1152]{1,0:T(8,128)(2,1)S(1)}, bf16[192,1152]{1,0:T(8,128)(2,1)S(1)}, u32[]{:S(2)}, u32[]{:S(2)}) collective-permute-start(bf16[192,1152]{1,0:T(8,128)(2,1)S(1)} %join.9.refs_0_.refs_5_), channel_id=1, source_target_pairs={{0,2},{1,3},{2,0},{3,1},{4,6},{5,7},{6,4},{7,5},{8,10},{9,11},{10,... | collective-permute-start | bytes 1327112 | tf_op jit(solution)/shard_map/ppermute | solution.py:427
  22.6 6.6 %collective-permute-start.12 = (bf16[96,1152]{1,0:T(8,128)(2,1)S(1)}, bf16[96,1152]{1,0:T(8,128)(2,1)S(1)}, u32[]{:S(2)}, u32[]{:S(2)}) collective-permute-start(bf16[96,1152]{1,0:T(8,128)(2,1)S(1)} %join.8.refs_0_), channel_id=1, source_target_pairs={{0,4},{1,5},{2,3},{3,2},{4,0},{5,1},{6,7},{7,6},{8,12},{9,13},{10,... | collective-permute-start | bytes 663560 | tf_op jit(solution)/shard_map/ppermute | solution.py:427
  23.1 9.6 %collective-permute-start.6 = (bf16[96,1152]{1,0:T(8,128)(2,1)S(1)}, bf16[96,1152]{1,0:T(8,128)(2,1)S(1)}, u32[]{:S(2)}, u32[]{:S(2)}) collective-permute-start(bf16[96,1152]{1,0:T(8,128)(2,1)S(1)} %join.6.refs_0_), channel_id=1, source_target_pairs={{0,4},{1,5},{2,3},{3,2},{4,0},{5,1},{6,7},{7,6},{8,12},{9,13},{10,... | collective-permute-start | bytes 663560 | tf_op jit(solution)/shard_map/ppermute | solution.py:427
  24.8 9.1 %collective-permute-start.5 = (bf16[96,1152]{1,0:T(8,128)(2,1)S(1)}, bf16[96,1152]{1,0:T(8,128)(2,1)S(1)}, u32[]{:S(2)}, u32[]{:S(2)}) collective-permute-start(bf16[96,1152]{1,0:T(8,128)(2,1)S(1)} %collective-permute-done.4.refs_1_), channel_id=1, source_target_pairs={{0,4},{1,5},{2,3},{3,2},{4,0},{5,1},{6,7},{7,6},{8,12},{9,13},{10,... | collective-permute-start | bytes 663560 | tf_op jit(solution)/shard_map/ppermute | solution.py:427
  26.0 10.2 %collective-permute-start.14 = (bf16[96,1152]{1,0:T(8,128)(2,1)S(1)}, bf16[96,1152]{1,0:T(8,128)(2,1)S(1)}, u32[]{:S(2)}, u32[]{:S(2)}) collective-permute-start(bf16[96,1152]{1,0:T(8,128)(2,1)S(1)} %collective-permute-done.10.refs_1_), channel_id=1, source_target_pairs={{0,4},{1,5},{2,3},{3,2},{4,0},{5,1},{6,7},{7,6},{8,12},{9,13},{10,... | collective-permute-start | bytes 663560 | tf_op jit(solution)/shard_map/ppermute | solution.py:427
  29.2 11.5 %collective-permute-start.13 = (bf16[192,1152]{1,0:T(8,128)(2,1)S(1)}, bf16[192,1152]{1,0:T(8,128)(2,1)S(1)}, u32[]{:S(2)}, u32[]{:S(2)}) collective-permute-start(bf16[192,1152]{1,0:T(8,128)(2,1)S(1)} %join.10.refs_0_.refs_10_.refs_12_), channel_id=1, source_target_pairs={{0,2},{1,3},{2,0},{3,1},{4,6},{5,7},{6,4},{7,5},{8,10},{9,11},{10,... | collective-permute-start | bytes 1327112 | tf_op jit(solution)/shard_map/ppermute | solution.py:427
  30.8 1.6 %copy-start.1 = (bf16[1024,1024]{1,0:T(8,128)(2,1)S(1)}, bf16[1024,1024]{1,0:T(8,128)(2,1)}, u32[]{:S(2)}) copy-start(bf16[1024,1024]{1,0:T(8,128)(2,1)} %b_ref.1) | copy-start | bytes 6291460
  33.9 18.3 %collective-permute-start.7 = (bf16[192,1152]{1,0:T(8,128)(2,1)S(1)}, bf16[192,1152]{1,0:T(8,128)(2,1)S(1)}, u32[]{:S(2)}, u32[]{:S(2)}) collective-permute-start(bf16[192,1152]{1,0:T(8,128)(2,1)S(1)} %join.7.refs_0_), channel_id=1, source_target_pairs={{0,2},{1,3},{2,0},{3,1},{4,6},{5,7},{6,4},{7,5},{8,10},{9,11},{10,... | collective-permute-start | bytes 1327112 | tf_op jit(solution)/shard_map/ppermute | solution.py:427
  36.3 10.3 %collective-permute-start.15 = (bf16[192,1152]{1,0:T(8,128)(2,1)S(1)}, bf16[192,1152]{1,0:T(8,128)(2,1)S(1)}, u32[]{:S(2)}, u32[]{:S(2)}) collective-permute-start(bf16[192,1152]{1,0:T(8,128)(2,1)S(1)} %join.11.refs_0_.refs_20_), channel_id=1, source_target_pairs={{0,2},{1,3},{2,0},{3,1},{4,6},{5,7},{6,4},{7,5},{8,10},{9,11},{10,... | collective-permute-start | bytes 1327112 | tf_op jit(solution)/shard_map/ppermute | solution.py:427

commit v2 on v1

--- a/solution.py
+++ b/solution.py
@@ -142,39 +142,65 @@
     return parts[0] if len(parts) == 1 else jnp.concatenate(parts, axis=0)
 
 
-def features(pays, w1_ref, w2_ref, ro_ref, hid_ref, grad_ref, inn_ref, right_ref):
-    rays, width = hid_ref.shape
-    extra = take(pays, 0, rays, slice(width, width + LANES)).astype(jnp.float32)
-    weight = extra[:, 0:1] + extra[:, 1:2] + extra[:, 2:3]
-    target = extra[:, 3:4] + extra[:, 4:5] + extra[:, 5:6]
-    pre = bdot(take(pays, 0, rays, slice(0, width)), w1_ref[...], ((1,), (0,)))
-    sig = sigmoid(pre)
-    slope_first = sig * (1.0 + pre * (1.0 - sig))
-    hidden = (pre * sig).astype(jnp.bfloat16)
-    hid_ref[...] = hidden
-    pre = bdot(hidden, w2_ref[...], ((1,), (0,)))
-    sig = sigmoid(pre)
-    readout = ro_ref[...]
-    signal = jnp.sum(pre * sig * readout, axis=1, keepdims=True)
-    grad = (weight * (sig * (1.0 + pre * (1.0 - sig))) * readout).astype(jnp.bfloat16)
-    grad_ref[...] = grad
-    carried = bdot(grad, w2_ref[...], ((1,), (1,)))
-    inn_ref[...] = (carried * slope_first).astype(jnp.bfloat16)
-    right_ref[...] = jnp.broadcast_to(weight * signal - target, (rays, LANES))
-
-
-def products(first, last, pays, inns, hids, grads, strip_ref, mirror_ref):
-    width = hids[0].shape[1]
-    whole = slice(0, width)
+def features(pays, w1, w2, ro):
+    width = w1.shape[0]
+    rays = sum(a.shape[0] for a in pays)
+
+    def kernel(*refs):
+        pay_refs, (w1_ref, w2_ref, ro_ref, out_ref) = refs[: len(pays)], refs[len(pays) :]
+        extra = take(pay_refs, 0, rays, slice(width, width + LANES)).astype(jnp.float32)
+        weight = extra[:, 0:1] + extra[:, 1:2] + extra[:, 2:3]
+        target = extra[:, 3:4] + extra[:, 4:5] + extra[:, 5:6]
+        value = take(pay_refs, 0, rays, slice(0, width))
+        out_ref[:, 0:width] = value
+        pre = bdot(value, w1_ref[...], ((1,), (0,)))
+        sig = sigmoid(pre)
+        slope_first = sig * (1.0 + pre * (1.0 - sig))
+        hidden = (pre * sig).astype(jnp.bfloat16)
+        out_ref[:, 2 * width : 3 * width] = hidden
+        pre = bdot(hidden, w2_ref[...], ((1,), (0,)))
+        sig = sigmoid(pre)
+        readout = ro_ref[...]
+        signal = jnp.sum(pre * sig * readout, axis=1, keepdims=True)
+        grad = (weight * (sig * (1.0 + pre * (1.0 - sig))) * readout).astype(jnp.bfloat16)
+        out_ref[:, 3 * width : 4 * width] = grad
+        carried = bdot(grad, w2_ref[...], ((1,), (1,)))
+        out_ref[:, width : 2 * width] = (carried * slope_first).astype(jnp.bfloat16)
+        terms = split3(weight * signal - target)
+        lane = lax.broadcasted_iota(jnp.int32, (rays, LANES), 1)
+        spread = jnp.zeros((rays, LANES), jnp.float32)
+        for k, term in enumerate(terms):
+            spread = jnp.where(lane == k, term, spread)
+        out_ref[:, 4 * width : 4 * width + LANES] = spread.astype(jnp.bfloat16)
+
+    vmem = pl.BlockSpec(memory_space=pltpu.VMEM)
+    units = w1.shape[1]
+    return pl.pallas_call(
+        kernel,
+        out_shape=jax.ShapeDtypeStruct((rays, 4 * width + LANES), jnp.bfloat16),
+        in_specs=[vmem] * (len(pays) + 3),
+        out_specs=vmem,
+        cost_estimate=pl.CostEstimate(
+            flops=6 * rays * width * units,
+            transcendentals=4 * rays * units,
+            bytes_accessed=8 * rays * width,
+        ),
+        compiler_params=pltpu.CompilerParams(vmem_limit_bytes=VMEM_BYTES),
+        name="features",
+    )(*pays, w1, w2, ro)
+
+
+def products(first, last, width, bundles, strip_ref, mirror_ref):
     nt = ((1,), (1,))
 
-    def pair(refs, r, c):
-        return bdot(take(refs, r * BLOCK, BLOCK, whole), take(refs, c * BLOCK, BLOCK, whole), nt)
+    def pair(k, r, c):
+        cols = slice(k * width, (k + 1) * width)
+        return bdot(take(bundles, r * BLOCK, BLOCK, cols), take(bundles, c * BLOCK, BLOCK, cols), nt)
 
     for r in range(first, last):
         rows = slice((r - first) * BLOCK, (r - first + 1) * BLOCK)
         for c in range(r + 1):
-            value = pair(pays, r, c) * pair(inns, r, c) + pair(hids, r, c) * pair(grads, r, c)
+            value = pair(0, r, c) * pair(1, r, c) + pair(2, r, c) * pair(3, r, c)
             strip_ref[rows, c * BLOCK : (c + 1) * BLOCK] = value
             if c < first:
                 mirror_ref[c * BLOCK : (c + 1) * BLOCK, rows] = value.T
@@ -183,9 +209,8 @@
                 strip_ref[other, r * BLOCK : (r + 1) * BLOCK] = value.T
 
 
-def finish(pays, inns, hids, grads, rights, strips, mirrors, own, out_ref, col_ref):
-    width = hids[0].shape[1]
-    total = sum(ref.shape[0] for ref in hids)
+def finish(width, bundles, strips, mirrors, own, out_ref, col_ref):
+    total = sum(ref.shape[0] for ref in bundles)
     tiles = total // LANES
 
     def to_columns(row):
@@ -233,24 +258,21 @@
     def dot(a, b):
         return jnp.sum(a * b, axis=1, keepdims=True)
 
-    right = jnp.concatenate(
-        [
-            ref[k * LANES : (k + 1) * LANES, :].T[0:1, :]
-            for ref in rights
-            for k in range(ref.shape[0] // LANES)
-        ],
-        axis=1,
-    )
+    offset = 0
+    for ref in bundles:
+        rows = slice(offset, offset + ref.shape[0])
+        col_ref[rows, :] = ref[:, 4 * width : 4 * width + LANES].astype(jnp.float32)
+        offset += ref.shape[0]
+    right = []
+    for t in range(tiles):
+        square = col_ref[t * LANES : (t + 1) * LANES, :].T
+        right.append(square[0:1, :] + square[1:2, :] + square[2:3, :])
+    right = jnp.concatenate(right, axis=1)
     answer = jnp.zeros_like(right)
     residual, direction = right, right
     norm_now = dot(right, right)
-    offset = 0
-    for ref in rights:
-        col_ref[offset : offset + ref.shape[0], :] = ref[...]
-        offset += ref.shape[0]
     for step in range(ITERS):
-        if step:
-            to_columns(direction)
+        to_columns(direction)
         image = apply(direction)
         alpha = norm_now / dot(direction, image)
         answer = answer + alpha * direction
@@ -264,16 +286,13 @@
     start = rank * own
     base = pl.multiple_of(start // LANES * LANES, LANES)
     shift = (LANES - (start - base)) % LANES
-    cols = pl.ds(base, LANES)
-    lane = None
+    lane = lax.broadcasted_iota(jnp.int32, (BLOCK, LANES), 1)
     sums = [jnp.zeros((LANES, width), jnp.float32)] * 2
-    offset = 0
-    for inn_ref, grad_ref, hid_ref in zip(inns, grads, hids):
-        rays = hid_ref.shape[0]
-        scale = col_ref[offset : offset + rays, :]
-        lane = lax.broadcasted_iota(jnp.int32, (rays, LANES), 1)
-        lefts = (take(pays, offset, rays, cols), hid_ref[:, cols])
-        for which, (left, ref) in enumerate(zip(lefts, (inn_ref, grad_ref))):
+    for r in range(total // BLOCK):
+        scale = col_ref[r * BLOCK : (r + 1) * BLOCK, :]
+        for which in range(2):
+            cols = pl.ds(pl.multiple_of(base + 2 * which * width, LANES), LANES)
+            left = take(bundles, r * BLOCK, BLOCK, cols)
             left = pltpu.roll(left.astype(jnp.float32) * scale, shift, 1)
             high = left.astype(jnp.bfloat16).astype(jnp.float32)
             rest = left - high
@@ -281,61 +300,50 @@
             low = rest - middle
             packed = jnp.where(lane < 2 * own, pltpu.roll(middle, own, 1), pltpu.roll(low, 2 * own, 1))
             packed = jnp.where(lane < own, high, packed).astype(jnp.bfloat16)
-            sums[which] = sums[which] + bdot(packed, ref[...], ((0,), (0,)))
-        offset += rays
+            cols = slice((2 * which + 1) * width, (2 * which + 2) * width)
+            other = take(bundles, r * BLOCK, BLOCK, cols)
+            sums[which] = sums[which] + bdot(packed, other, ((0,), (0,)))
     for which, value in enumerate(sums):
         value = value[0:own] + value[own : 2 * own] + value[2 * own : 3 * own]
         out_ref[:, which * width : (which + 1) * width] = -LEARN * value
 
 
-def stage(k, count, pays, w1, w2, ro, before, own):
-    width, units = w1.shape
-    rays = sum(a.shape[0] for a in pays)
+def stage(k, count, bundles, before, width, own):
+    total = sum(a.shape[0] for a in bundles)
+    rays = total // (k + 1)
     first, last = k * rays // BLOCK, (k + 1) * rays // BLOCK
     final = k + 1 == count
-    rows, cols = (last - first) * BLOCK, last * BLOCK
-    made = [((rays, units), jnp.bfloat16)] * 3 + [((rays, LANES), jnp.float32)]
-    made.append(((rows, cols), jnp.float32))
+    rows = (last - first) * BLOCK
+    made = [((rows, last * BLOCK), jnp.float32)]
     if first:
         made.append(((first * BLOCK, rows), jnp.float32))
-    operands, spots = [], []
-
-    def place(arrays):
-        spots.append((len(operands), len(operands) + len(arrays)))
-        operands.extend(arrays)
-
-    place([*pays, w1, w2, ro])
-    for done in before:
-        place(done["pays"])
-        place(done["made"] if final else done["made"][:3])
+    old = [a for arrays in before for a in arrays] if final else []
+    operands = [*bundles, *old]
 
     def kernel(*refs):
-        groups = [list(refs[a:b]) for a, b in spots]
+        every = refs[: len(bundles)]
+        earlier = list(refs[len(bundles) : len(operands)])
         tail = list(refs[len(operands) :])
         out_ref = tail.pop(0) if final else None
-        mine = tail[: len(made)]
-        own_pays = groups[0][: len(pays)]
-        features(own_pays, *groups[0][len(pays) :], *mine[:4])
-        old_pays = [ref for group in groups[1::2] for ref in group]
-        hids, grads, inns = ([g[i] for g in groups[2::2]] + [mine[i]] for i in range(3))
-        every = [*old_pays, *own_pays]
-        products(first, last, every, inns, hids, grads, mine[4], mine[5] if first else None)
+        strip, mirror = tail[0], tail[1] if first else None
+        products(first, last, width, every, strip, mirror)
         if final:
-            rights, strips = ([g[i] for g in groups[2::2]] + [mine[i]] for i in (3, 4))
-            mirrors = [g[5] if len(g) > 5 else None for g in groups[2::2] + [mine]]
-            finish(every, inns, hids, grads, rights, strips, mirrors, own, out_ref, tail[-1])
+            strips, mirrors = [], []
+            for arrays in before:
+                strips.append(earlier.pop(0))
+                mirrors.append(earlier.pop(0) if len(arrays) > 1 else None)
+            finish(width, every, [*strips, strip], [*mirrors, mirror], own, out_ref, tail[-1])
 
     vmem = pl.BlockSpec(memory_space=pltpu.VMEM)
     if final:
         out_shape = jax.ShapeDtypeStruct((own, 2 * width), jnp.float32)
         out_specs = vmem
         scratch = [pltpu.VMEM(*m) for m in made]
-        scratch.append(pltpu.VMEM((count * rays, LANES), jnp.float32))
+        scratch.append(pltpu.VMEM((total, LANES), jnp.float32))
     else:
         out_shape = [jax.ShapeDtypeStruct(*m) for m in made]
         out_specs = [vmem] * len(made)
         scratch = []
-    flops = 6 * rays * width * units + 4 * width * (last * last - first * first) * BLOCK * BLOCK
     return pl.pallas_call(
         kernel,
         out_shape=out_shape,
@@ -343,7 +351,9 @@
         out_specs=out_specs,
         scratch_shapes=scratch,
         cost_estimate=pl.CostEstimate(
-            flops=flops, transcendentals=4 * rays * units, bytes_accessed=8 * rays * width
+            flops=4 * width * (last * last - first * first) * BLOCK * BLOCK,
+            transcendentals=0,
+            bytes_accessed=8 * rays * width,
         ),
         compiler_params=pltpu.CompilerParams(vmem_limit_bytes=VMEM_BYTES),
     )(*operands)
@@ -442,18 +452,13 @@
         two.append(swap(base[k], crossed))
         three.append(swap(one[k], crossed))
     parts = ((base[0], one[0]), (base[1], two[0]), (three[0], one[1]), (three[1], two[1]))
-    halves = []
-    for both in parts:
-        halves.append(join(both))
     ro = readout.astype(jnp.float32)[None, :]
-    before = []
-    for k, half in enumerate(halves):
-        pays = [half, swap(half, ((1, 0),) * 2)]
-        got = stage(
-            k, len(halves), pays, first_weight, second_weight, ro, before, width // (n_row * n_col)
-        )
-        before.append({"pays": pays, "made": got})
-    return got
+    bundles, before = [], []
+    for k, both in enumerate(parts):
+        mine = features(both, first_weight, second_weight, ro)
+        bundles += [mine, swap(mine, ((1, 0),) * 2)]
+        before.append(stage(k, len(parts), list(bundles), before, width, width // (n_row * n_col)))
+    return before[-1]
 
 
 def solution(mesh):

time: 69.3 us -> 65.4 us (0.944)
  waiting for transfers between devices: 14.9 us -> 7.46 us
  starting transfers between devices: 17.5 us -> 22 us
  Pallas kernels: 32.6 us -> 30.3 us
    pallas_call x4, Pallas kernels: 32 us -> 20.5 us  [stage(): pl.pallas_call(kernel, out_shape=out_shape, in_specs=[vmem] * len(operand...]
    pallas_call x0 -> x4, Pallas kernels: none -> 8.44 us  [features(): pl.pallas_call(kernel, out_shape=jax.ShapeDtypeStruct((rays, 4 * width +...]
    ppermute x16, waiting for transfers between devices: 14.9 us -> 7.46 us  [swap(): return lax.ppermute(value, ('row', 'col'), pairs)]
    ppermute x16, starting transfers between devices: 17.5 us -> 22 us  [swap(): return lax.ppermute(value, ('row', 'col'), pairs)]
    pallas_call x6 -> x2, Pallas kernels: 0.32 us -> 1.09 us  [join(): pl.pallas_call(kernel, out_shape=jax.ShapeDtypeStruct((rows, wide), piece...]
    unnamed x8 -> x4, local copies, waits for them, and re-layouts: 2.49 us -> 3.18 us
  transfers between devices with their start and end apart: 16 -> 16, of which waited for: 7 -> 4; matrix products, arithmetic and copies ran while one was open for 2% -> 3% of each run, Pallas kernels for 23% -> 23%
where the time goes in v2:
time: 65.4 us; the launch traced here: 65.2 us
  Pallas kernels  30.3 us (46%)
  starting transfers between devices  22 us (34%)
  waiting for transfers between devices  7.46 us (11%)
  local copies, waits for them, and re-layouts  3.18 us (5%)
  other arithmetic  2.13 us (3%)
    ppermute x16, starting transfers between devices, swap(): return lax.ppermute(value, ('row', 'col'), pairs)  22 us
    pallas_call x4, Pallas kernels, stage(): pl.pallas_call(kernel, out_shape=out_shape, in_specs=[vmem] * len(operand...  20.5 us
    pallas_call x4, Pallas kernels, features(): pl.pallas_call(kernel, out_shape=jax.ShapeDtypeStruct((rays, 4 * width +...  8.44 us
    ppermute x16, waiting for transfers between devices, swap(): return lax.ppermute(value, ('row', 'col'), pairs)  7.46 us
    unnamed x4, local copies, waits for them, and re-layouts  3.18 us
  transfers between devices with their start and end apart: 16, of which 4 were waited for; matrix products, arithmetic and copies ran while one was open for 3% of the time, Pallas kernels for 23%

profile of v2, /device:TPU:1, one launch (start us, length us, event | category | flops | bytes accessed | tf_op | source)
XLA Modules:
  0.0 65.2 jit_solution(8372270062359937047)
XLA Ops:
  0.0 2.1 %collective-permute-start = (bf16[48,1024]{1,0:T(8,128)(2,1)}, bf16[48,1024]{1,0:T(8,128)(2,1)S(1)}, u32[]{:S(2)}, u32[]{:S(2)}) collective-permute-start(bf16[48,1024]{1,0:T(8,128)(2,1)} %refs_0_.1), channel_id=1, source_target_pairs={{0,8},{1,9},{2,10},{3,11},{4,12},{5,13},{6,14},{7,15},{8,0},{9,1},... | collective-permute-start | bytes 294920 | tf_op jit(solution)/shard_map/ppermute | solution.py:437
  2.1 0.7 %add_multiply_fusion = f32[48]{0:T(128)S(1)} fusion(s32[48]{0:T(128)} %param.13, s32[48]{0:T(128)} %param.12), kind=kLoop, calls=%fused_computation.1 | loop fusion | flops 336 | bytes 576 | tf_op jit(solution)/shard_map/mul | solution.py:28
  2.8 0.7 %broadcast_select_fusion.refs_2_ = f32[2,48]{1,0:T(2,128)S(1)} fusion(pred[2]{0:T(512)(128)(4,1)S(1)} %iota_compare_fusion, f32[48]{0:T(128)} %param.11, f32[48]{0:T(128)S(1)} %add_multiply_fusion), kind=kLoop, calls=%fused_computation | loop fusion | flops 96 | bytes 770 | tf_op jit(solution)/shard_map/jit(_where)/select_n | solution.py:440
  3.6 2.4 %collective-permute-done.1.refs_3_ = f32[2,48]{1,0:T(2,128)S(1)} collective-permute-done((f32[2,48]{1,0:T(2,128)S(1)}, f32[2,48]{1,0:T(2,128)S(1)}, u32[]{:S(2)}, u32[]{:S(2)}) %collective-permute-start.1) | collective-permute-done | bytes 416 | tf_op jit(solution)/shard_map/ppermute | solution.py:437
  6.0 1.0 %join.2.refs_0_ = bf16[96,1152]{1,0:T(8,128)(2,1)S(1)} custom-call(bf16[48,1024]{1,0:T(8,128)(2,1)} %refs_0_.1, bf16[48,1024]{1,0:T(8,128)(2,1)S(1)} %collective-permute-done.refs_1_, f32[2,48]{1,0:T(2,128)S(1)} %broadcast_select_fusion.refs_2_, f32[2,48]{1,0:T(2,128)S(1)} %collective-permute-done.1.refs_3_), custom_call_target="tpu_custom_call" | custom-call | tf_op jit(solution)/shard_map/join/pallas_call | solution.py:393
  7.0 1.3 %collective-permute-start.2 = (bf16[96,1152]{1,0:T(8,128)(2,1)S(1)}, bf16[96,1152]{1,0:T(8,128)(2,1)S(1)}, u32[]{:S(2)}, u32[]{:S(2)}) collective-permute-start(bf16[96,1152]{1,0:T(8,128)(2,1)S(1)} %join.2.refs_0_), channel_id=1, source_target_pairs={{0,1},{1,0},{2,6},{3,7},{4,5},{5,4},{6,2},{7,3},{8,9},{9,8},{10,14... | collective-permute-start | bytes 663560 | tf_op jit(solution)/shard_map/ppermute | solution.py:437
  8.3 1.2 %collective-permute-start.8 = (bf16[96,1152]{1,0:T(8,128)(2,1)S(1)}, bf16[96,1152]{1,0:T(8,128)(2,1)S(1)}, u32[]{:S(2)}, u32[]{:S(2)}) collective-permute-start(bf16[96,1152]{1,0:T(8,128)(2,1)S(1)} %join.2.refs_0_), channel_id=1, source_target_pairs={{0,4},{1,5},{2,3},{3,2},{4,0},{5,1},{6,7},{7,6},{8,12},{9,13},{10,... | collective-permute-start | bytes 663560 | tf_op jit(solution)/shard_map/ppermute | solution.py:437
  9.5 2.5 %collective-permute-start.5 = (bf16[48,1024]{1,0:T(8,128)(2,1)}, bf16[48,1024]{1,0:T(8,128)(2,1)S(1)}, u32[]{:S(2)}, u32[]{:S(2)}) collective-permute-start(bf16[48,1024]{1,0:T(8,128)(2,1)} %refs_0_.1), channel_id=1, source_target_pairs={{0,24},{1,25},{2,26},{3,27},{4,28},{5,29},{6,30},{7,31},{8,16},{9,... | collective-permute-start | bytes 294920 | tf_op jit(solution)/shard_map/ppermute | solution.py:437
  12.0 2.2 %collective-permute-start.7 = (f32[2,48]{1,0:T(2,128)S(1)}, f32[2,48]{1,0:T(2,128)S(1)}, u32[]{:S(2)}, u32[]{:S(2)}) collective-permute-start(f32[2,48]{1,0:T(2,128)S(1)} %broadcast_select_fusion.refs_2_), channel_id=1, source_target_pairs={{0,24},{1,25},{2,26},{3,27},{4,28},{5,29},{6,30},{7,31},{8,16},{9,... | collective-permute-start | bytes 1160 | tf_op jit(solution)/shard_map/ppermute | solution.py:437
  14.2 2.2 %collective-permute-done.7.refs_3_ = f32[2,48]{1,0:T(2,128)S(1)} collective-permute-done((f32[2,48]{1,0:T(2,128)S(1)}, f32[2,48]{1,0:T(2,128)S(1)}, u32[]{:S(2)}, u32[]{:S(2)}) %collective-permute-start.7) | collective-permute-done | bytes 416 | tf_op jit(solution)/shard_map/ppermute | solution.py:437
  16.4 5.6 %collective-permute-start.6 = (f32[2,48]{1,0:T(2,128)S(1)}, f32[2,48]{1,0:T(2,128)S(1)}, u32[]{:S(2)}, u32[]{:S(2)}) collective-permute-start(f32[2,48]{1,0:T(2,128)S(1)} %broadcast_select_fusion.refs_2_), channel_id=1, source_target_pairs={{0,16},{1,17},{2,18},{3,19},{4,20},{5,21},{6,22},{7,23},{8,24},{9,... | collective-permute-start | bytes 1160 | tf_op jit(solution)/shard_map/ppermute | solution.py:437
  22.0 0.7 %broadcast_in_dim.27 = f32[1024]{0:T(1024)S(1)} convert(bf16[1024]{0:T(1024)(128)(2,1)} %param.10) | non-fusion elementwise | flops 1024 | bytes 6144 | tf_op jit(solution)/shard_map/broadcast_in_dim | solution.py:455
  22.7 1.6 %copy-done = bf16[1024,1024]{1,0:T(8,128)(2,1)S(1)} copy-done((bf16[1024,1024]{1,0:T(8,128)(2,1)S(1)}, bf16[1024,1024]{1,0:T(8,128)(2,1)}, u32[]{:S(2)}) %copy-start) | copy-done | bytes 2097176
  24.3 1.6 %copy-done.1 = bf16[1024,1024]{1,0:T(8,128)(2,1)S(1)} copy-done((bf16[1024,1024]{1,0:T(8,128)(2,1)S(1)}, bf16[1024,1024]{1,0:T(8,128)(2,1)}, u32[]{:S(2)}) %copy-start.1) | copy-done | bytes 2097176
  25.9 0.3 load.1
  26.3 0.3 collective-permute-start.11
  26.6 0.3 collective-permute-start.10
  26.9 2.1 %features.4.refs_0_ = bf16[192,4224]{1,0:T(8,128)(2,1)S(1)} custom-call(bf16[96,1152]{1,0:T(8,128)(2,1)S(1)} %join.2.refs_0_, bf16[96,1152]{1,0:T(8,128)(2,1)S(1)} %collective-permute-done.2.refs_1_, bf16[1024,1024]{1,0:T(8,128)(2,1)S(1)} %get-tuple-element.11.refs_2_, bf16[1024,1024]{1,0:T(8,128)(2,1)S(1)} %get-tuple-element.12.refs_3_, f32[1,1024]{1,0:T(1,128)S(1)} %bitcast.1), custom_call_target="tpu_custom_call" | custom-call | flops 1207959552 | bytes 1572864 | tf_op jit(solution)/shard_map/features/pallas_call | solution.py:178
  29.0 2.5 %collective-permute-start.3 = (bf16[192,4224]{1,0:T(8,128)(2,1)S(1)}, bf16[192,4224]{1,0:T(8,128)(2,1)S(1)}, u32[]{:S(2)}, u32[]{:S(2)}) collective-permute-start(bf16[192,4224]{1,0:T(8,128)(2,1)S(1)} %features.4.refs_0_), channel_id=1, source_target_pairs={{0,2},{1,3},{2,0},{3,1},{4,6},{5,7},{6,4},{7,5},{8,10},{9,11},{10,... | collective-permute-start | bytes 4866056 | tf_op jit(solution)/shard_map/ppermute | solution.py:437
  31.5 2.1 %features.5.refs_2_ = bf16[192,4224]{1,0:T(8,128)(2,1)S(1)} custom-call(bf16[96,1152]{1,0:T(8,128)(2,1)S(1)} %join.3.refs_0_, bf16[96,1152]{1,0:T(8,128)(2,1)S(1)} %collective-permute-done.8.refs_1_, bf16[1024,1024]{1,0:T(8,128)(2,1)S(1)} %get-tuple-element.11.refs_2_, bf16[1024,1024]{1,0:T(8,128)(2,1)S(1)} %get-tuple-element.12.refs_3_, f32[1,1024]{1,0:T(1,128)S(1)} %bitcast.2), custom_call_target="tpu_custom_call" | custom-call | flops 1207959552 | bytes 1572864 | tf_op jit(solution)/shard_map/features/pallas_call | solution.py:178
  33.7 1.3 %collective-permute-start.14 = (bf16[96,1152]{1,0:T(8,128)(2,1)S(1)}, bf16[96,1152]{1,0:T(8,128)(2,1)S(1)}, u32[]{:S(2)}, u32[]{:S(2)}) collective-permute-start(bf16[96,1152]{1,0:T(8,128)(2,1)S(1)} %join.3.refs_0_), channel_id=1, source_target_pairs={{0,4},{1,5},{2,3},{3,2},{4,0},{5,1},{6,7},{7,6},{8,12},{9,13},{10,... | collective-permute-start | bytes 663560 | tf_op jit(solution)/shard_map/ppermute | solution.py:437
  35.0 0.2 collective-permute-start.13
  35.2 2.1 %features.6.refs_4_ = bf16[192,4224]{1,0:T(8,128)(2,1)S(1)} custom-call(bf16[96,1152]{1,0:T(8,128)(2,1)S(1)} %collective-permute-done.10.refs_0_, bf16[96,1152]{1,0:T(8,128)(2,1)S(1)} %collective-permute-done.11.refs_1_, bf16[1024,1024]{1,0:T(8,128)(2,1)S(1)} %get-tuple-element.11.refs_2_, bf16[1024,1024]{1,0:T(8,128)(2,1)S(1)} %get-tuple-element.12.refs_3_, ...), custom_call_target="tpu_custom_call" | custom-call | flops 1207959552 | bytes 1572864 | tf_op jit(solution)/shard_map/features/pallas_call | solution.py:178
  37.3 1.1 %collective-permute-start.12 = (bf16[192,4224]{1,0:T(8,128)(2,1)S(1)}, bf16[192,4224]{1,0:T(8,128)(2,1)S(1)}, u32[]{:S(2)}, u32[]{:S(2)}) collective-permute-start(bf16[192,4224]{1,0:T(8,128)(2,1)S(1)} %features.6.refs_4_), channel_id=1, source_target_pairs={{0,2},{1,3},{2,0},{3,1},{4,6},{5,7},{6,4},{7,5},{8,10},{9,11},{10,... | collective-permute-start | bytes 4866056 | tf_op jit(solution)/shard_map/ppermute | solution.py:437
  38.4 0.4 collective-permute-done.14.refs_1_
  38.8 2.4 %collective-permute-done.13.refs_0_ = bf16[96,1152]{1,0:T(8,128)(2,1)S(1)} collective-permute-done((bf16[96,1152]{1,0:T(8,128)(2,1)S(1)}, bf16[96,1152]{1,0:T(8,128)(2,1)S(1)}, u32[]{:S(2)}, u32[]{:S(2)}) %collective-permute-start.13) | collective-permute-done | bytes 221216 | tf_op jit(solution)/shard_map/ppermute | solution.py:437
  41.2 2.1 %features.7.refs_6_ = bf16[192,4224]{1,0:T(8,128)(2,1)S(1)} custom-call(bf16[96,1152]{1,0:T(8,128)(2,1)S(1)} %collective-permute-done.13.refs_0_, bf16[96,1152]{1,0:T(8,128)(2,1)S(1)} %collective-permute-done.14.refs_1_, bf16[1024,1024]{1,0:T(8,128)(2,1)S(1)} %get-tuple-element.11.refs_2_, bf16[1024,1024]{1,0:T(8,128)(2,1)S(1)} %get-tuple-element.12.refs_3_, ...), custom_call_target="tpu_custom_call" | custom-call | flops 1207959552 | bytes 1572864 | tf_op jit(solution)/shard_map/features/pallas_call | solution.py:178
  43.3 1.4 %collective-permute-start.15 = (bf16[192,4224]{1,0:T(8,128)(2,1)S(1)}, bf16[192,4224]{1,0:T(8,128)(2,1)S(1)}, u32[]{:S(2)}, u32[]{:S(2)}) collective-permute-start(bf16[192,4224]{1,0:T(8,128)(2,1)S(1)} %features.7.refs_6_), channel_id=1, source_target_pairs={{0,2},{1,3},{2,0},{3,1},{4,6},{5,7},{6,4},{7,5},{8,10},{9,11},{10,... | collective-permute-start | bytes 4866056 | tf_op jit(solution)/shard_map/ppermute | solution.py:437
  44.7 0.7 %shard_map.73.refs_8_ = f32[256,256]{1,0:T(8,128)S(1)} custom-call(bf16[192,4224]{1,0:T(8,128)(2,1)S(1)} %features.4.refs_0_, bf16[192,4224]{1,0:T(8,128)(2,1)S(1)} %collective-permute-done.3.refs_1_), custom_call_target="tpu_custom_call" | custom-call | flops 268435456 | bytes 3145728 | tf_op jit(solution)/shard_map/pallas_call | solution.py:347
  45.4 2.9 %shard_map.74 = (f32[512,768]{1,0:T(8,128)S(1)}, f32[256,512]{1,0:T(8,128)S(1)}) custom-call(bf16[192,4224]{1,0:T(8,128)(2,1)S(1)} %features.4.refs_0_, bf16[192,4224]{1,0:T(8,128)(2,1)S(1)} %collective-permute-done.3.refs_1_, bf16[192,4224]{1,0:T(8,128)(2,1)S(1)} %features.5.refs_2_, bf16[192,4224]{1,0:T(8,128)(2,1)S(1)} %collective-permute-done.9.refs_3_), custom_call_target="tpu_custom_call" | custom-call | flops 2147483648 | bytes 3145728 | tf_op jit(solution)/shard_map/pallas_call | solution.py:347
  48.4 2.4 %shard_map.75 = (f32[256,1024]{1,0:T(8,128)S(1)}, f32[768,256]{1,0:T(8,128)S(1)}) custom-call(bf16[192,4224]{1,0:T(8,128)(2,1)S(1)} %features.4.refs_0_, bf16[192,4224]{1,0:T(8,128)(2,1)S(1)} %collective-permute-done.3.refs_1_, bf16[192,4224]{1,0:T(8,128)(2,1)S(1)} %features.5.refs_2_, bf16[192,4224]{1,0:T(8,128)(2,1)S(1)} %collective-permute-done.9.refs_3_, ...), custom_call_target="tpu_custom_call" | custom-call | flops 1879048192 | bytes 3145728 | tf_op jit(solution)/shard_map/pallas_call | solution.py:347
  50.7 14.4 %shard_map.76 = f32[32,2048]{1,0:T(8,128)} custom-call(bf16[192,4224]{1,0:T(8,128)(2,1)S(1)} %features.4.refs_0_, bf16[192,4224]{1,0:T(8,128)(2,1)S(1)} %collective-permute-done.3.refs_1_, bf16[192,4224]{1,0:T(8,128)(2,1)S(1)} %features.5.refs_2_, bf16[192,4224]{1,0:T(8,128)(2,1)S(1)} %collective-permute-done.9.refs_3_, ...), custom_call_target="tpu_custom_call" | custom-call | flops 5368709120 | bytes 3145728 | tf_op jit(solution)/shard_map/pallas_call | solution.py:347
  (19 shorter events, 0.2 us)
Async XLA Ops:
  0.0 6.0 %collective-permute-start = (bf16[48,1024]{1,0:T(8,128)(2,1)}, bf16[48,1024]{1,0:T(8,128)(2,1)S(1)}, u32[]{:S(2)}, u32[]{:S(2)}) collective-permute-start(bf16[48,1024]{1,0:T(8,128)(2,1)} %refs_0_.1), channel_id=1, source_target_pairs={{0,8},{1,9},{2,10},{3,11},{4,12},{5,13},{6,14},{7,15},{8,0},{9,1},... | collective-permute-start | bytes 294920 | tf_op jit(solution)/shard_map/ppermute | solution.py:437
  3.6 2.4 %collective-permute-start.1 = (f32[2,48]{1,0:T(2,128)S(1)}, f32[2,48]{1,0:T(2,128)S(1)}, u32[]{:S(2)}, u32[]{:S(2)}) collective-permute-start(f32[2,48]{1,0:T(2,128)S(1)} %broadcast_select_fusion.refs_2_), channel_id=1, source_target_pairs={{0,8},{1,9},{2,10},{3,11},{4,12},{5,13},{6,14},{7,15},{8,0},{9,1},... | collective-permute-start | bytes 1160 | tf_op jit(solution)/shard_map/ppermute | solution.py:437
  7.0 19.6 %collective-permute-start.2 = (bf16[96,1152]{1,0:T(8,128)(2,1)S(1)}, bf16[96,1152]{1,0:T(8,128)(2,1)S(1)}, u32[]{:S(2)}, u32[]{:S(2)}) collective-permute-start(bf16[96,1152]{1,0:T(8,128)(2,1)S(1)} %join.2.refs_0_), channel_id=1, source_target_pairs={{0,1},{1,0},{2,6},{3,7},{4,5},{5,4},{6,2},{7,3},{8,9},{9,8},{10,14... | collective-permute-start | bytes 663560 | tf_op jit(solution)/shard_map/ppermute | solution.py:437
  8.3 23.2 %collective-permute-start.8 = (bf16[96,1152]{1,0:T(8,128)(2,1)S(1)}, bf16[96,1152]{1,0:T(8,128)(2,1)S(1)}, u32[]{:S(2)}, u32[]{:S(2)}) collective-permute-start(bf16[96,1152]{1,0:T(8,128)(2,1)S(1)} %join.2.refs_0_), channel_id=1, source_target_pairs={{0,4},{1,5},{2,3},{3,2},{4,0},{5,1},{6,7},{7,6},{8,12},{9,13},{10,... | collective-permute-start | bytes 663560 | tf_op jit(solution)/shard_map/ppermute | solution.py:437
  9.5 16.7 %collective-permute-start.5 = (bf16[48,1024]{1,0:T(8,128)(2,1)}, bf16[48,1024]{1,0:T(8,128)(2,1)S(1)}, u32[]{:S(2)}, u32[]{:S(2)}) collective-permute-start(bf16[48,1024]{1,0:T(8,128)(2,1)} %refs_0_.1), channel_id=1, source_target_pairs={{0,24},{1,25},{2,26},{3,27},{4,28},{5,29},{6,30},{7,31},{8,16},{9,... | collective-permute-start | bytes 294920 | tf_op jit(solution)/shard_map/ppermute | solution.py:437
  12.0 14.2 %collective-permute-start.4 = (bf16[48,1024]{1,0:T(8,128)(2,1)}, bf16[48,1024]{1,0:T(8,128)(2,1)S(1)}, u32[]{:S(2)}, u32[]{:S(2)}) collective-permute-start(bf16[48,1024]{1,0:T(8,128)(2,1)} %refs_0_.1), channel_id=1, source_target_pairs={{0,16},{1,17},{2,18},{3,19},{4,20},{5,21},{6,22},{7,23},{8,24},{9,... | collective-permute-start | bytes 294920 | tf_op jit(solution)/shard_map/ppermute | solution.py:437
  12.0 4.4 %collective-permute-start.7 = (f32[2,48]{1,0:T(2,128)S(1)}, f32[2,48]{1,0:T(2,128)S(1)}, u32[]{:S(2)}, u32[]{:S(2)}) collective-permute-start(f32[2,48]{1,0:T(2,128)S(1)} %broadcast_select_fusion.refs_2_), channel_id=1, source_target_pairs={{0,24},{1,25},{2,26},{3,27},{4,28},{5,29},{6,30},{7,31},{8,16},{9,... | collective-permute-start | bytes 1160 | tf_op jit(solution)/shard_map/ppermute | solution.py:437
  16.4 9.8 %collective-permute-start.6 = (f32[2,48]{1,0:T(2,128)S(1)}, f32[2,48]{1,0:T(2,128)S(1)}, u32[]{:S(2)}, u32[]{:S(2)}) collective-permute-start(f32[2,48]{1,0:T(2,128)S(1)} %broadcast_select_fusion.refs_2_), channel_id=1, source_target_pairs={{0,16},{1,17},{2,18},{3,19},{4,20},{5,21},{6,22},{7,23},{8,24},{9,... | collective-permute-start | bytes 1160 | tf_op jit(solution)/shard_map/ppermute | solution.py:437
  22.7 1.6 %copy-start = (bf16[1024,1024]{1,0:T(8,128)(2,1)S(1)}, bf16[1024,1024]{1,0:T(8,128)(2,1)}, u32[]{:S(2)}) copy-start(bf16[1024,1024]{1,0:T(8,128)(2,1)} %a_ref.1) | copy-start | bytes 6291460
  24.3 1.6 %copy-start.1 = (bf16[1024,1024]{1,0:T(8,128)(2,1)S(1)}, bf16[1024,1024]{1,0:T(8,128)(2,1)}, u32[]{:S(2)}) copy-start(bf16[1024,1024]{1,0:T(8,128)(2,1)} %b_ref.1) | copy-start | bytes 6291460
  26.3 8.6 %collective-permute-start.11 = (bf16[96,1152]{1,0:T(8,128)(2,1)S(1)}, bf16[96,1152]{1,0:T(8,128)(2,1)S(1)}, u32[]{:S(2)}, u32[]{:S(2)}) collective-permute-start(bf16[96,1152]{1,0:T(8,128)(2,1)S(1)} %join.3.refs_0_), channel_id=1, source_target_pairs={{0,1},{1,0},{2,6},{3,7},{4,5},{5,4},{6,2},{7,3},{8,9},{9,8},{10,14... | collective-permute-start | bytes 663560 | tf_op jit(solution)/shard_map/ppermute | solution.py:437
  26.6 8.6 %collective-permute-start.10 = (bf16[96,1152]{1,0:T(8,128)(2,1)S(1)}, bf16[96,1152]{1,0:T(8,128)(2,1)S(1)}, u32[]{:S(2)}, u32[]{:S(2)}) collective-permute-start(bf16[96,1152]{1,0:T(8,128)(2,1)S(1)} %collective-permute-done.2.refs_1_), channel_id=1, source_target_pairs={{0,4},{1,5},{2,3},{3,2},{4,0},{5,1},{6,7},{7,6},{8,12},{9,13},{10,... | collective-permute-start | bytes 663560 | tf_op jit(solution)/shard_map/ppermute | solution.py:437
  29.0 15.7 %collective-permute-start.3 = (bf16[192,4224]{1,0:T(8,128)(2,1)S(1)}, bf16[192,4224]{1,0:T(8,128)(2,1)S(1)}, u32[]{:S(2)}, u32[]{:S(2)}) collective-permute-start(bf16[192,4224]{1,0:T(8,128)(2,1)S(1)} %features.4.refs_0_), channel_id=1, source_target_pairs={{0,2},{1,3},{2,0},{3,1},{4,6},{5,7},{6,4},{7,5},{8,10},{9,11},{10,... | collective-permute-start | bytes 4866056 | tf_op jit(solution)/shard_map/ppermute | solution.py:437
  33.6 11.8 %collective-permute-start.9 = (bf16[192,4224]{1,0:T(8,128)(2,1)S(1)}, bf16[192,4224]{1,0:T(8,128)(2,1)S(1)}, u32[]{:S(2)}, u32[]{:S(2)}) collective-permute-start(bf16[192,4224]{1,0:T(8,128)(2,1)S(1)} %features.5.refs_2_), channel_id=1, source_target_pairs={{0,2},{1,3},{2,0},{3,1},{4,6},{5,7},{6,4},{7,5},{8,10},{9,11},{10,... | collective-permute-start | bytes 4866056 | tf_op jit(solution)/shard_map/ppermute | solution.py:437
  33.7 5.1 %collective-permute-start.14 = (bf16[96,1152]{1,0:T(8,128)(2,1)S(1)}, bf16[96,1152]{1,0:T(8,128)(2,1)S(1)}, u32[]{:S(2)}, u32[]{:S(2)}) collective-permute-start(bf16[96,1152]{1,0:T(8,128)(2,1)S(1)} %join.3.refs_0_), channel_id=1, source_target_pairs={{0,4},{1,5},{2,3},{3,2},{4,0},{5,1},{6,7},{7,6},{8,12},{9,13},{10,... | collective-permute-start | bytes 663560 | tf_op jit(solution)/shard_map/ppermute | solution.py:437
  35.0 6.2 %collective-permute-start.13 = (bf16[96,1152]{1,0:T(8,128)(2,1)S(1)}, bf16[96,1152]{1,0:T(8,128)(2,1)S(1)}, u32[]{:S(2)}, u32[]{:S(2)}) collective-permute-start(bf16[96,1152]{1,0:T(8,128)(2,1)S(1)} %collective-permute-done.11.refs_1_), channel_id=1, source_target_pairs={{0,4},{1,5},{2,3},{3,2},{4,0},{5,1},{6,7},{7,6},{8,12},{9,13},{10,... | collective-permute-start | bytes 663560 | tf_op jit(solution)/shard_map/ppermute | solution.py:437
  37.3 11.0 %collective-permute-start.12 = (bf16[192,4224]{1,0:T(8,128)(2,1)S(1)}, bf16[192,4224]{1,0:T(8,128)(2,1)S(1)}, u32[]{:S(2)}, u32[]{:S(2)}) collective-permute-start(bf16[192,4224]{1,0:T(8,128)(2,1)S(1)} %features.6.refs_4_), channel_id=1, source_target_pairs={{0,2},{1,3},{2,0},{3,1},{4,6},{5,7},{6,4},{7,5},{8,10},{9,11},{10,... | collective-permute-start | bytes 4866056 | tf_op jit(solution)/shard_map/ppermute | solution.py:437
  43.3 7.4 %collective-permute-start.15 = (bf16[192,4224]{1,0:T(8,128)(2,1)S(1)}, bf16[192,4224]{1,0:T(8,128)(2,1)S(1)}, u32[]{:S(2)}, u32[]{:S(2)}) collective-permute-start(bf16[192,4224]{1,0:T(8,128)(2,1)S(1)} %features.7.refs_6_), channel_id=1, source_target_pairs={{0,2},{1,3},{2,0},{3,1},{4,6},{5,7},{6,4},{7,5},{8,10},{9,11},{10,... | collective-permute-start | bytes 4866056 | tf_op jit(solution)/shard_map/ppermute | solution.py:437

commit v3 on v2

--- a/solution.py
+++ b/solution.py
@@ -287,7 +287,7 @@
     base = pl.multiple_of(start // LANES * LANES, LANES)
     shift = (LANES - (start - base)) % LANES
     lane = lax.broadcasted_iota(jnp.int32, (BLOCK, LANES), 1)
-    sums = [jnp.zeros((LANES, width), jnp.float32)] * 2
+    lefts = [[], []]
     for r in range(total // BLOCK):
         scale = col_ref[r * BLOCK : (r + 1) * BLOCK, :]
         for which in range(2):
@@ -300,10 +300,10 @@
             low = rest - middle
             packed = jnp.where(lane < 2 * own, pltpu.roll(middle, own, 1), pltpu.roll(low, 2 * own, 1))
             packed = jnp.where(lane < own, high, packed).astype(jnp.bfloat16)
-            cols = slice((2 * which + 1) * width, (2 * which + 2) * width)
-            other = take(bundles, r * BLOCK, BLOCK, cols)
-            sums[which] = sums[which] + bdot(packed, other, ((0,), (0,)))
-    for which, value in enumerate(sums):
+            lefts[which].append(packed)
+    for which, left in enumerate(lefts):
+        cols = slice((2 * which + 1) * width, (2 * which + 2) * width)
+        value = bdot(jnp.concatenate(left, axis=0), take(bundles, 0, total, cols), ((0,), (0,)))
         value = value[0:own] + value[own : 2 * own] + value[2 * own : 3 * own]
         out_ref[:, which * width : (which + 1) * width] = -LEARN * value
 

time: 65.4 us -> 64.8 us (level)
  no operation moved by 1% of the time
where the time goes in v3:
time: 64.8 us; the launch traced here: 64.5 us
  Pallas kernels  29.7 us (46%)
  starting transfers between devices  22 us (34%)
  waiting for transfers between devices  7.46 us (12%)
  local copies, waits for them, and re-layouts  3.18 us (5%)
  other arithmetic  2.13 us (3%)
    ppermute x16, starting transfers between devices, swap(): return lax.ppermute(value, ('row', 'col'), pairs)  22 us
    pallas_call x4, Pallas kernels, stage(): pl.pallas_call(kernel, out_shape=out_shape, in_specs=[vmem] * len(operand...  19.8 us
    pallas_call x4, Pallas kernels, features(): pl.pallas_call(kernel, out_shape=jax.ShapeDtypeStruct((rays, 4 * width +...  8.44 us
    ppermute x16, waiting for transfers between devices, swap(): return lax.ppermute(value, ('row', 'col'), pairs)  7.46 us
    unnamed x4, local copies, waits for them, and re-layouts  3.18 us
  transfers between devices with their start and end apart: 16, of which 4 were waited for; matrix products, arithmetic and copies ran while one was open for 3% of the time, Pallas kernels for 23%

profile of v3, /device:TPU:1, one launch (start us, length us, event | category | flops | bytes accessed | tf_op | source)
XLA Modules:
  0.0 64.5 jit_solution(15053283285054678504)
XLA Ops:
  0.0 2.1 %collective-permute-start = (bf16[48,1024]{1,0:T(8,128)(2,1)}, bf16[48,1024]{1,0:T(8,128)(2,1)S(1)}, u32[]{:S(2)}, u32[]{:S(2)}) collective-permute-start(bf16[48,1024]{1,0:T(8,128)(2,1)} %refs_0_.1), channel_id=1, source_target_pairs={{0,8},{1,9},{2,10},{3,11},{4,12},{5,13},{6,14},{7,15},{8,0},{9,1},... | collective-permute-start | bytes 294920 | tf_op jit(solution)/shard_map/ppermute | solution.py:437
  2.1 0.7 %add_multiply_fusion = f32[48]{0:T(128)S(1)} fusion(s32[48]{0:T(128)} %param.13, s32[48]{0:T(128)} %param.12), kind=kLoop, calls=%fused_computation.1 | loop fusion | flops 336 | bytes 576 | tf_op jit(solution)/shard_map/mul | solution.py:28
  2.8 0.7 %broadcast_select_fusion.refs_2_ = f32[2,48]{1,0:T(2,128)S(1)} fusion(pred[2]{0:T(512)(128)(4,1)S(1)} %iota_compare_fusion, f32[48]{0:T(128)} %param.11, f32[48]{0:T(128)S(1)} %add_multiply_fusion), kind=kLoop, calls=%fused_computation | loop fusion | flops 96 | bytes 770 | tf_op jit(solution)/shard_map/jit(_where)/select_n | solution.py:440
  3.6 2.4 %collective-permute-done.1.refs_3_ = f32[2,48]{1,0:T(2,128)S(1)} collective-permute-done((f32[2,48]{1,0:T(2,128)S(1)}, f32[2,48]{1,0:T(2,128)S(1)}, u32[]{:S(2)}, u32[]{:S(2)}) %collective-permute-start.1) | collective-permute-done | bytes 416 | tf_op jit(solution)/shard_map/ppermute | solution.py:437
  6.0 1.0 %join.2.refs_0_ = bf16[96,1152]{1,0:T(8,128)(2,1)S(1)} custom-call(bf16[48,1024]{1,0:T(8,128)(2,1)} %refs_0_.1, bf16[48,1024]{1,0:T(8,128)(2,1)S(1)} %collective-permute-done.refs_1_, f32[2,48]{1,0:T(2,128)S(1)} %broadcast_select_fusion.refs_2_, f32[2,48]{1,0:T(2,128)S(1)} %collective-permute-done.1.refs_3_), custom_call_target="tpu_custom_call" | custom-call | tf_op jit(solution)/shard_map/join/pallas_call | solution.py:393
  7.0 1.3 %collective-permute-start.2 = (bf16[96,1152]{1,0:T(8,128)(2,1)S(1)}, bf16[96,1152]{1,0:T(8,128)(2,1)S(1)}, u32[]{:S(2)}, u32[]{:S(2)}) collective-permute-start(bf16[96,1152]{1,0:T(8,128)(2,1)S(1)} %join.2.refs_0_), channel_id=1, source_target_pairs={{0,1},{1,0},{2,6},{3,7},{4,5},{5,4},{6,2},{7,3},{8,9},{9,8},{10,14... | collective-permute-start | bytes 663560 | tf_op jit(solution)/shard_map/ppermute | solution.py:437
  8.3 1.2 %collective-permute-start.8 = (bf16[96,1152]{1,0:T(8,128)(2,1)S(1)}, bf16[96,1152]{1,0:T(8,128)(2,1)S(1)}, u32[]{:S(2)}, u32[]{:S(2)}) collective-permute-start(bf16[96,1152]{1,0:T(8,128)(2,1)S(1)} %join.2.refs_0_), channel_id=1, source_target_pairs={{0,4},{1,5},{2,3},{3,2},{4,0},{5,1},{6,7},{7,6},{8,12},{9,13},{10,... | collective-permute-start | bytes 663560 | tf_op jit(solution)/shard_map/ppermute | solution.py:437
  9.5 2.5 %collective-permute-start.5 = (bf16[48,1024]{1,0:T(8,128)(2,1)}, bf16[48,1024]{1,0:T(8,128)(2,1)S(1)}, u32[]{:S(2)}, u32[]{:S(2)}) collective-permute-start(bf16[48,1024]{1,0:T(8,128)(2,1)} %refs_0_.1), channel_id=1, source_target_pairs={{0,24},{1,25},{2,26},{3,27},{4,28},{5,29},{6,30},{7,31},{8,16},{9,... | collective-permute-start | bytes 294920 | tf_op jit(solution)/shard_map/ppermute | solution.py:437
  12.0 2.2 %collective-permute-start.7 = (f32[2,48]{1,0:T(2,128)S(1)}, f32[2,48]{1,0:T(2,128)S(1)}, u32[]{:S(2)}, u32[]{:S(2)}) collective-permute-start(f32[2,48]{1,0:T(2,128)S(1)} %broadcast_select_fusion.refs_2_), channel_id=1, source_target_pairs={{0,24},{1,25},{2,26},{3,27},{4,28},{5,29},{6,30},{7,31},{8,16},{9,... | collective-permute-start | bytes 1160 | tf_op jit(solution)/shard_map/ppermute | solution.py:437
  14.2 2.2 %collective-permute-done.7.refs_3_ = f32[2,48]{1,0:T(2,128)S(1)} collective-permute-done((f32[2,48]{1,0:T(2,128)S(1)}, f32[2,48]{1,0:T(2,128)S(1)}, u32[]{:S(2)}, u32[]{:S(2)}) %collective-permute-start.7) | collective-permute-done | bytes 416 | tf_op jit(solution)/shard_map/ppermute | solution.py:437
  16.4 5.6 %collective-permute-start.6 = (f32[2,48]{1,0:T(2,128)S(1)}, f32[2,48]{1,0:T(2,128)S(1)}, u32[]{:S(2)}, u32[]{:S(2)}) collective-permute-start(f32[2,48]{1,0:T(2,128)S(1)} %broadcast_select_fusion.refs_2_), channel_id=1, source_target_pairs={{0,16},{1,17},{2,18},{3,19},{4,20},{5,21},{6,22},{7,23},{8,24},{9,... | collective-permute-start | bytes 1160 | tf_op jit(solution)/shard_map/ppermute | solution.py:437
  22.0 0.7 %broadcast_in_dim.27 = f32[1024]{0:T(1024)S(1)} convert(bf16[1024]{0:T(1024)(128)(2,1)} %param.10) | non-fusion elementwise | flops 1024 | bytes 6144 | tf_op jit(solution)/shard_map/broadcast_in_dim | solution.py:455
  22.7 1.6 %copy-done = bf16[1024,1024]{1,0:T(8,128)(2,1)S(1)} copy-done((bf16[1024,1024]{1,0:T(8,128)(2,1)S(1)}, bf16[1024,1024]{1,0:T(8,128)(2,1)}, u32[]{:S(2)}) %copy-start) | copy-done | bytes 2097176
  24.3 1.6 %copy-done.1 = bf16[1024,1024]{1,0:T(8,128)(2,1)S(1)} copy-done((bf16[1024,1024]{1,0:T(8,128)(2,1)S(1)}, bf16[1024,1024]{1,0:T(8,128)(2,1)}, u32[]{:S(2)}) %copy-start.1) | copy-done | bytes 2097176
  25.9 0.3 load.1
  26.3 0.3 collective-permute-start.11
  26.6 0.3 collective-permute-start.10
  26.9 2.1 %features.4.refs_0_ = bf16[192,4224]{1,0:T(8,128)(2,1)S(1)} custom-call(bf16[96,1152]{1,0:T(8,128)(2,1)S(1)} %join.2.refs_0_, bf16[96,1152]{1,0:T(8,128)(2,1)S(1)} %collective-permute-done.2.refs_1_, bf16[1024,1024]{1,0:T(8,128)(2,1)S(1)} %get-tuple-element.11.refs_2_, bf16[1024,1024]{1,0:T(8,128)(2,1)S(1)} %get-tuple-element.12.refs_3_, f32[1,1024]{1,0:T(1,128)S(1)} %bitcast.1), custom_call_target="tpu_custom_call" | custom-call | flops 1207959552 | bytes 1572864 | tf_op jit(solution)/shard_map/features/pallas_call | solution.py:178
  29.0 2.5 %collective-permute-start.3 = (bf16[192,4224]{1,0:T(8,128)(2,1)S(1)}, bf16[192,4224]{1,0:T(8,128)(2,1)S(1)}, u32[]{:S(2)}, u32[]{:S(2)}) collective-permute-start(bf16[192,4224]{1,0:T(8,128)(2,1)S(1)} %features.4.refs_0_), channel_id=1, source_target_pairs={{0,2},{1,3},{2,0},{3,1},{4,6},{5,7},{6,4},{7,5},{8,10},{9,11},{10,... | collective-permute-start | bytes 4866056 | tf_op jit(solution)/shard_map/ppermute | solution.py:437
  31.5 2.1 %features.5.refs_2_ = bf16[192,4224]{1,0:T(8,128)(2,1)S(1)} custom-call(bf16[96,1152]{1,0:T(8,128)(2,1)S(1)} %join.3.refs_0_, bf16[96,1152]{1,0:T(8,128)(2,1)S(1)} %collective-permute-done.8.refs_1_, bf16[1024,1024]{1,0:T(8,128)(2,1)S(1)} %get-tuple-element.11.refs_2_, bf16[1024,1024]{1,0:T(8,128)(2,1)S(1)} %get-tuple-element.12.refs_3_, f32[1,1024]{1,0:T(1,128)S(1)} %bitcast.2), custom_call_target="tpu_custom_call" | custom-call | flops 1207959552 | bytes 1572864 | tf_op jit(solution)/shard_map/features/pallas_call | solution.py:178
  33.7 1.3 %collective-permute-start.14 = (bf16[96,1152]{1,0:T(8,128)(2,1)S(1)}, bf16[96,1152]{1,0:T(8,128)(2,1)S(1)}, u32[]{:S(2)}, u32[]{:S(2)}) collective-permute-start(bf16[96,1152]{1,0:T(8,128)(2,1)S(1)} %join.3.refs_0_), channel_id=1, source_target_pairs={{0,4},{1,5},{2,3},{3,2},{4,0},{5,1},{6,7},{7,6},{8,12},{9,13},{10,... | collective-permute-start | bytes 663560 | tf_op jit(solution)/shard_map/ppermute | solution.py:437
  35.0 0.2 collective-permute-start.13
  35.2 2.1 %features.6.refs_4_ = bf16[192,4224]{1,0:T(8,128)(2,1)S(1)} custom-call(bf16[96,1152]{1,0:T(8,128)(2,1)S(1)} %collective-permute-done.10.refs_0_, bf16[96,1152]{1,0:T(8,128)(2,1)S(1)} %collective-permute-done.11.refs_1_, bf16[1024,1024]{1,0:T(8,128)(2,1)S(1)} %get-tuple-element.11.refs_2_, bf16[1024,1024]{1,0:T(8,128)(2,1)S(1)} %get-tuple-element.12.refs_3_, ...), custom_call_target="tpu_custom_call" | custom-call | flops 1207959552 | bytes 1572864 | tf_op jit(solution)/shard_map/features/pallas_call | solution.py:178
  37.3 1.1 %collective-permute-start.12 = (bf16[192,4224]{1,0:T(8,128)(2,1)S(1)}, bf16[192,4224]{1,0:T(8,128)(2,1)S(1)}, u32[]{:S(2)}, u32[]{:S(2)}) collective-permute-start(bf16[192,4224]{1,0:T(8,128)(2,1)S(1)} %features.6.refs_4_), channel_id=1, source_target_pairs={{0,2},{1,3},{2,0},{3,1},{4,6},{5,7},{6,4},{7,5},{8,10},{9,11},{10,... | collective-permute-start | bytes 4866056 | tf_op jit(solution)/shard_map/ppermute | solution.py:437
  38.4 0.4 collective-permute-done.14.refs_1_
  38.8 2.4 %collective-permute-done.13.refs_0_ = bf16[96,1152]{1,0:T(8,128)(2,1)S(1)} collective-permute-done((bf16[96,1152]{1,0:T(8,128)(2,1)S(1)}, bf16[96,1152]{1,0:T(8,128)(2,1)S(1)}, u32[]{:S(2)}, u32[]{:S(2)}) %collective-permute-start.13) | collective-permute-done | bytes 221216 | tf_op jit(solution)/shard_map/ppermute | solution.py:437
  41.2 2.1 %features.7.refs_6_ = bf16[192,4224]{1,0:T(8,128)(2,1)S(1)} custom-call(bf16[96,1152]{1,0:T(8,128)(2,1)S(1)} %collective-permute-done.13.refs_0_, bf16[96,1152]{1,0:T(8,128)(2,1)S(1)} %collective-permute-done.14.refs_1_, bf16[1024,1024]{1,0:T(8,128)(2,1)S(1)} %get-tuple-element.11.refs_2_, bf16[1024,1024]{1,0:T(8,128)(2,1)S(1)} %get-tuple-element.12.refs_3_, ...), custom_call_target="tpu_custom_call" | custom-call | flops 1207959552 | bytes 1572864 | tf_op jit(solution)/shard_map/features/pallas_call | solution.py:178
  43.3 1.4 %collective-permute-start.15 = (bf16[192,4224]{1,0:T(8,128)(2,1)S(1)}, bf16[192,4224]{1,0:T(8,128)(2,1)S(1)}, u32[]{:S(2)}, u32[]{:S(2)}) collective-permute-start(bf16[192,4224]{1,0:T(8,128)(2,1)S(1)} %features.7.refs_6_), channel_id=1, source_target_pairs={{0,2},{1,3},{2,0},{3,1},{4,6},{5,7},{6,4},{7,5},{8,10},{9,11},{10,... | collective-permute-start | bytes 4866056 | tf_op jit(solution)/shard_map/ppermute | solution.py:437
  44.7 0.7 %shard_map.73.refs_8_ = f32[256,256]{1,0:T(8,128)S(1)} custom-call(bf16[192,4224]{1,0:T(8,128)(2,1)S(1)} %features.4.refs_0_, bf16[192,4224]{1,0:T(8,128)(2,1)S(1)} %collective-permute-done.3.refs_1_), custom_call_target="tpu_custom_call" | custom-call | flops 268435456 | bytes 3145728 | tf_op jit(solution)/shard_map/pallas_call | solution.py:347
  45.4 2.9 %shard_map.74 = (f32[512,768]{1,0:T(8,128)S(1)}, f32[256,512]{1,0:T(8,128)S(1)}) custom-call(bf16[192,4224]{1,0:T(8,128)(2,1)S(1)} %features.4.refs_0_, bf16[192,4224]{1,0:T(8,128)(2,1)S(1)} %collective-permute-done.3.refs_1_, bf16[192,4224]{1,0:T(8,128)(2,1)S(1)} %features.5.refs_2_, bf16[192,4224]{1,0:T(8,128)(2,1)S(1)} %collective-permute-done.9.refs_3_), custom_call_target="tpu_custom_call" | custom-call | flops 2147483648 | bytes 3145728 | tf_op jit(solution)/shard_map/pallas_call | solution.py:347
  48.4 2.4 %shard_map.75 = (f32[256,1024]{1,0:T(8,128)S(1)}, f32[768,256]{1,0:T(8,128)S(1)}) custom-call(bf16[192,4224]{1,0:T(8,128)(2,1)S(1)} %features.4.refs_0_, bf16[192,4224]{1,0:T(8,128)(2,1)S(1)} %collective-permute-done.3.refs_1_, bf16[192,4224]{1,0:T(8,128)(2,1)S(1)} %features.5.refs_2_, bf16[192,4224]{1,0:T(8,128)(2,1)S(1)} %collective-permute-done.9.refs_3_, ...), custom_call_target="tpu_custom_call" | custom-call | flops 1879048192 | bytes 3145728 | tf_op jit(solution)/shard_map/pallas_call | solution.py:347
  50.7 13.8 %shard_map.76 = f32[32,2048]{1,0:T(8,128)} custom-call(bf16[192,4224]{1,0:T(8,128)(2,1)S(1)} %features.4.refs_0_, bf16[192,4224]{1,0:T(8,128)(2,1)S(1)} %collective-permute-done.3.refs_1_, bf16[192,4224]{1,0:T(8,128)(2,1)S(1)} %features.5.refs_2_, bf16[192,4224]{1,0:T(8,128)(2,1)S(1)} %collective-permute-done.9.refs_3_, ...), custom_call_target="tpu_custom_call" | custom-call | flops 5368709120 | bytes 3145728 | tf_op jit(solution)/shard_map/pallas_call | solution.py:347
  (19 shorter events, 0.2 us)
Async XLA Ops:
  0.0 6.0 %collective-permute-start = (bf16[48,1024]{1,0:T(8,128)(2,1)}, bf16[48,1024]{1,0:T(8,128)(2,1)S(1)}, u32[]{:S(2)}, u32[]{:S(2)}) collective-permute-start(bf16[48,1024]{1,0:T(8,128)(2,1)} %refs_0_.1), channel_id=1, source_target_pairs={{0,8},{1,9},{2,10},{3,11},{4,12},{5,13},{6,14},{7,15},{8,0},{9,1},... | collective-permute-start | bytes 294920 | tf_op jit(solution)/shard_map/ppermute | solution.py:437
  3.6 2.4 %collective-permute-start.1 = (f32[2,48]{1,0:T(2,128)S(1)}, f32[2,48]{1,0:T(2,128)S(1)}, u32[]{:S(2)}, u32[]{:S(2)}) collective-permute-start(f32[2,48]{1,0:T(2,128)S(1)} %broadcast_select_fusion.refs_2_), channel_id=1, source_target_pairs={{0,8},{1,9},{2,10},{3,11},{4,12},{5,13},{6,14},{7,15},{8,0},{9,1},... | collective-permute-start | bytes 1160 | tf_op jit(solution)/shard_map/ppermute | solution.py:437
  7.0 19.6 %collective-permute-start.2 = (bf16[96,1152]{1,0:T(8,128)(2,1)S(1)}, bf16[96,1152]{1,0:T(8,128)(2,1)S(1)}, u32[]{:S(2)}, u32[]{:S(2)}) collective-permute-start(bf16[96,1152]{1,0:T(8,128)(2,1)S(1)} %join.2.refs_0_), channel_id=1, source_target_pairs={{0,1},{1,0},{2,6},{3,7},{4,5},{5,4},{6,2},{7,3},{8,9},{9,8},{10,14... | collective-permute-start | bytes 663560 | tf_op jit(solution)/shard_map/ppermute | solution.py:437
  8.3 23.2 %collective-permute-start.8 = (bf16[96,1152]{1,0:T(8,128)(2,1)S(1)}, bf16[96,1152]{1,0:T(8,128)(2,1)S(1)}, u32[]{:S(2)}, u32[]{:S(2)}) collective-permute-start(bf16[96,1152]{1,0:T(8,128)(2,1)S(1)} %join.2.refs_0_), channel_id=1, source_target_pairs={{0,4},{1,5},{2,3},{3,2},{4,0},{5,1},{6,7},{7,6},{8,12},{9,13},{10,... | collective-permute-start | bytes 663560 | tf_op jit(solution)/shard_map/ppermute | solution.py:437
  9.5 16.7 %collective-permute-start.5 = (bf16[48,1024]{1,0:T(8,128)(2,1)}, bf16[48,1024]{1,0:T(8,128)(2,1)S(1)}, u32[]{:S(2)}, u32[]{:S(2)}) collective-permute-start(bf16[48,1024]{1,0:T(8,128)(2,1)} %refs_0_.1), channel_id=1, source_target_pairs={{0,24},{1,25},{2,26},{3,27},{4,28},{5,29},{6,30},{7,31},{8,16},{9,... | collective-permute-start | bytes 294920 | tf_op jit(solution)/shard_map/ppermute | solution.py:437
  12.0 14.2 %collective-permute-start.4 = (bf16[48,1024]{1,0:T(8,128)(2,1)}, bf16[48,1024]{1,0:T(8,128)(2,1)S(1)}, u32[]{:S(2)}, u32[]{:S(2)}) collective-permute-start(bf16[48,1024]{1,0:T(8,128)(2,1)} %refs_0_.1), channel_id=1, source_target_pairs={{0,16},{1,17},{2,18},{3,19},{4,20},{5,21},{6,22},{7,23},{8,24},{9,... | collective-permute-start | bytes 294920 | tf_op jit(solution)/shard_map/ppermute | solution.py:437
  12.0 4.4 %collective-permute-start.7 = (f32[2,48]{1,0:T(2,128)S(1)}, f32[2,48]{1,0:T(2,128)S(1)}, u32[]{:S(2)}, u32[]{:S(2)}) collective-permute-start(f32[2,48]{1,0:T(2,128)S(1)} %broadcast_select_fusion.refs_2_), channel_id=1, source_target_pairs={{0,24},{1,25},{2,26},{3,27},{4,28},{5,29},{6,30},{7,31},{8,16},{9,... | collective-permute-start | bytes 1160 | tf_op jit(solution)/shard_map/ppermute | solution.py:437
  16.4 9.8 %collective-permute-start.6 = (f32[2,48]{1,0:T(2,128)S(1)}, f32[2,48]{1,0:T(2,128)S(1)}, u32[]{:S(2)}, u32[]{:S(2)}) collective-permute-start(f32[2,48]{1,0:T(2,128)S(1)} %broadcast_select_fusion.refs_2_), channel_id=1, source_target_pairs={{0,16},{1,17},{2,18},{3,19},{4,20},{5,21},{6,22},{7,23},{8,24},{9,... | collective-permute-start | bytes 1160 | tf_op jit(solution)/shard_map/ppermute | solution.py:437
  22.7 1.6 %copy-start = (bf16[1024,1024]{1,0:T(8,128)(2,1)S(1)}, bf16[1024,1024]{1,0:T(8,128)(2,1)}, u32[]{:S(2)}) copy-start(bf16[1024,1024]{1,0:T(8,128)(2,1)} %a_ref.1) | copy-start | bytes 6291460
  24.3 1.6 %copy-start.1 = (bf16[1024,1024]{1,0:T(8,128)(2,1)S(1)}, bf16[1024,1024]{1,0:T(8,128)(2,1)}, u32[]{:S(2)}) copy-start(bf16[1024,1024]{1,0:T(8,128)(2,1)} %b_ref.1) | copy-start | bytes 6291460
  26.3 8.6 %collective-permute-start.11 = (bf16[96,1152]{1,0:T(8,128)(2,1)S(1)}, bf16[96,1152]{1,0:T(8,128)(2,1)S(1)}, u32[]{:S(2)}, u32[]{:S(2)}) collective-permute-start(bf16[96,1152]{1,0:T(8,128)(2,1)S(1)} %join.3.refs_0_), channel_id=1, source_target_pairs={{0,1},{1,0},{2,6},{3,7},{4,5},{5,4},{6,2},{7,3},{8,9},{9,8},{10,14... | collective-permute-start | bytes 663560 | tf_op jit(solution)/shard_map/ppermute | solution.py:437
  26.6 8.6 %collective-permute-start.10 = (bf16[96,1152]{1,0:T(8,128)(2,1)S(1)}, bf16[96,1152]{1,0:T(8,128)(2,1)S(1)}, u32[]{:S(2)}, u32[]{:S(2)}) collective-permute-start(bf16[96,1152]{1,0:T(8,128)(2,1)S(1)} %collective-permute-done.2.refs_1_), channel_id=1, source_target_pairs={{0,4},{1,5},{2,3},{3,2},{4,0},{5,1},{6,7},{7,6},{8,12},{9,13},{10,... | collective-permute-start | bytes 663560 | tf_op jit(solution)/shard_map/ppermute | solution.py:437
  29.0 15.7 %collective-permute-start.3 = (bf16[192,4224]{1,0:T(8,128)(2,1)S(1)}, bf16[192,4224]{1,0:T(8,128)(2,1)S(1)}, u32[]{:S(2)}, u32[]{:S(2)}) collective-permute-start(bf16[192,4224]{1,0:T(8,128)(2,1)S(1)} %features.4.refs_0_), channel_id=1, source_target_pairs={{0,2},{1,3},{2,0},{3,1},{4,6},{5,7},{6,4},{7,5},{8,10},{9,11},{10,... | collective-permute-start | bytes 4866056 | tf_op jit(solution)/shard_map/ppermute | solution.py:437
  33.6 11.8 %collective-permute-start.9 = (bf16[192,4224]{1,0:T(8,128)(2,1)S(1)}, bf16[192,4224]{1,0:T(8,128)(2,1)S(1)}, u32[]{:S(2)}, u32[]{:S(2)}) collective-permute-start(bf16[192,4224]{1,0:T(8,128)(2,1)S(1)} %features.5.refs_2_), channel_id=1, source_target_pairs={{0,2},{1,3},{2,0},{3,1},{4,6},{5,7},{6,4},{7,5},{8,10},{9,11},{10,... | collective-permute-start | bytes 4866056 | tf_op jit(solution)/shard_map/ppermute | solution.py:437
  33.7 5.1 %collective-permute-start.14 = (bf16[96,1152]{1,0:T(8,128)(2,1)S(1)}, bf16[96,1152]{1,0:T(8,128)(2,1)S(1)}, u32[]{:S(2)}, u32[]{:S(2)}) collective-permute-start(bf16[96,1152]{1,0:T(8,128)(2,1)S(1)} %join.3.refs_0_), channel_id=1, source_target_pairs={{0,4},{1,5},{2,3},{3,2},{4,0},{5,1},{6,7},{7,6},{8,12},{9,13},{10,... | collective-permute-start | bytes 663560 | tf_op jit(solution)/shard_map/ppermute | solution.py:437
  35.0 6.2 %collective-permute-start.13 = (bf16[96,1152]{1,0:T(8,128)(2,1)S(1)}, bf16[96,1152]{1,0:T(8,128)(2,1)S(1)}, u32[]{:S(2)}, u32[]{:S(2)}) collective-permute-start(bf16[96,1152]{1,0:T(8,128)(2,1)S(1)} %collective-permute-done.11.refs_1_), channel_id=1, source_target_pairs={{0,4},{1,5},{2,3},{3,2},{4,0},{5,1},{6,7},{7,6},{8,12},{9,13},{10,... | collective-permute-start | bytes 663560 | tf_op jit(solution)/shard_map/ppermute | solution.py:437
  37.3 11.0 %collective-permute-start.12 = (bf16[192,4224]{1,0:T(8,128)(2,1)S(1)}, bf16[192,4224]{1,0:T(8,128)(2,1)S(1)}, u32[]{:S(2)}, u32[]{:S(2)}) collective-permute-start(bf16[192,4224]{1,0:T(8,128)(2,1)S(1)} %features.6.refs_4_), channel_id=1, source_target_pairs={{0,2},{1,3},{2,0},{3,1},{4,6},{5,7},{6,4},{7,5},{8,10},{9,11},{10,... | collective-permute-start | bytes 4866056 | tf_op jit(solution)/shard_map/ppermute | solution.py:437
  43.3 7.4 %collective-permute-start.15 = (bf16[192,4224]{1,0:T(8,128)(2,1)S(1)}, bf16[192,4224]{1,0:T(8,128)(2,1)S(1)}, u32[]{:S(2)}, u32[]{:S(2)}) collective-permute-start(bf16[192,4224]{1,0:T(8,128)(2,1)S(1)} %features.7.refs_6_), channel_id=1, source_target_pairs={{0,2},{1,3},{2,0},{3,1},{4,6},{5,7},{6,4},{7,5},{8,10},{9,11},{10,... | collective-permute-start | bytes 4866056 | tf_op jit(solution)/shard_map/ppermute | solution.py:437
